TPU v7x, 512 devices: a whole 4x4x16 slice. The times are simulated.
512 devices in a mesh: grp: 64 (over z, x_lo, core), tp: 8 (over x_hi, y).
Axes of the slice: x: 4 (x_hi: 2, x_lo: 2; x = x_hi * 2 + x_lo), y: 4, z: 16, core: 2. Of those that a mesh axis runs over, the one named last changes fastest.
Arguments:
- memory_rows: bfloat16 [65536, 4096], P('grp', 'tp'), may hold values from -24 to 24, as said below
- norm_gain: float32 [4096], replicated, may hold values from 0.25 to 1.75
- key_weight: bfloat16 [4096, 4096], P(None, 'tp'), may hold values from -0.09375 to 0.09375
- owner_table: int32 [8192], replicated, may hold values from 0 to 8191, as said below
Outputs:
- placed_keys: bfloat16 [65536, 4096], P('grp', 'tp')
Inputs may be any that keep to these rules, and one draw needn't show every extreme that they name: A permutation of the 8192 block numbers. Block b of the input goes to block position owner_table[b], which lies in group owner_table[b] // 128. The 128 blocks of one group go to all 64 groups, exactly 2 blocks to each of them. `memory_rows`: rows have offsets and scales of their own, and features a common pattern.
All inputs are finite; a program needn't handle non-finite values.
Results may differ from a plain program's by a relative error of at most 0.0049.
Values may be sent and summed in bfloat16 or wider, within the bound.
No kernel may reach another device: no remote copies, remote signals or barrier semaphores. Data moves between devices by JAX's collectives and lax.ppermute only.
A program may use at most 64 MiB of HBM per device.

v0:
```python
import jax
import jax.numpy as jnp
from jax import lax
from jax.sharding import PartitionSpec as P

BLK_ROWS = 8


EPS = 1e-05


def to_owners(block_rows, owner_table):
    groups = lax.axis_size("grp")
    position = lax.axis_index("grp")
    row_count, col_count = block_rows.shape
    blocks_here = row_count // BLK_ROWS
    capacity = max(1, blocks_here // groups)
    owned_slots = lax.dynamic_slice_in_dim(owner_table, position * blocks_here, blocks_here)
    target = owned_slots // blocks_here
    block_ids = jnp.arange(blocks_here, dtype=jnp.int32)
    earlier = (target[None, :] == target[:, None]) & (block_ids[None, :] < block_ids[:, None])
    rank = jnp.sum(earlier.astype(jnp.int32), axis=1)
    send_slot = target * capacity + rank
    slot_ids = jnp.arange(groups * capacity, dtype=jnp.int32)
    sender = (send_slot[None, :] == slot_ids[:, None]).astype(jnp.bfloat16)
    flattened = block_rows.reshape(blocks_here, BLK_ROWS * col_count)
    outgoing = jnp.dot(sender, flattened, preferred_element_type=jnp.float32).astype(jnp.bfloat16)
    incoming = lax.all_to_all(outgoing, "grp", split_axis=0, concat_axis=0, tiled=True)
    block_total = owner_table.shape[0]
    inverse = (
        jnp.zeros((block_total,), jnp.int32)
        .at[owner_table]
        .set(jnp.arange(block_total, dtype=jnp.int32))
    )
    arriving = lax.dynamic_slice_in_dim(inverse, position * blocks_here, blocks_here)
    anchor_group = arriving // blocks_here
    anchor_column = arriving % blocks_here
    target_table = owner_table.reshape(groups, blocks_here) // blocks_here
    anchor_targets = target_table[anchor_group]
    before = (anchor_targets == position) & (block_ids[None, :] < anchor_column[:, None])
    anchor_rank = jnp.sum(before.astype(jnp.int32), axis=1)
    source_slot = anchor_group * capacity + anchor_rank
    picker = (source_slot[:, None] == slot_ids[None, :]).astype(jnp.bfloat16)
    placed = jnp.dot(picker, incoming, preferred_element_type=jnp.float32).astype(jnp.bfloat16)
    return placed.reshape(row_count, col_count)


def project(memory_rows, norm_gain, key_weight):
    width = norm_gain.shape[0]
    whole_rows = lax.all_gather(memory_rows, "tp", axis=1, tiled=True)
    values = whole_rows.astype(jnp.float32)
    row_mean = jnp.sum(values, axis=1, keepdims=True) / width
    row_var = jnp.sum(values * values, axis=1, keepdims=True) / width - row_mean * row_mean
    normed = ((values - row_mean) * lax.rsqrt(row_var + EPS) * norm_gain[None, :]).astype(
        jnp.bfloat16
    )
    keys = jnp.dot(normed, key_weight, preferred_element_type=jnp.float32)
    return keys.astype(jnp.bfloat16)


def on_device(memory_rows, norm_gain, key_weight, owner_table):
    keys = project(memory_rows, norm_gain, key_weight)
    return to_owners(keys, owner_table)


def solution(mesh):
    in_specs = (P("grp", "tp"), P(), P(None, "tp"), P())
    out_specs = P("grp", "tp")
    return jax.shard_map(
        on_device, mesh=mesh, in_specs=in_specs, out_specs=out_specs, check_vma=False
    )
```

profile of v0, /device:TPU:2, one launch (start us, length us, event | category | flops | bytes accessed | tf_op | source)
XLA Modules:
  0.0 236.6 jit_solution(608830909230115830)
XLA Ops:
  6.5 0.0 all-gather.2.cloned.1.call-start
  6.5 0.7 all-gather.2.cloned.1.call-update
  7.3 0.8 and_select_fusion
  8.0 0.2 convert_reduce_fusion.1
  8.2 0.8 multiply_add_fusion
  9.0 132.8 %all-gather.2.cloned.1.call-done = bf16[1024,4096]{1,0:T(8,128)(2,1)} async-done(((bf16[1024,512]{1,0:T(8,128)(2,1)}), bf16[1024,4096]{1,0:T(8,128)(2,1)}) %all-gather.2.cloned.1.call-update) | async-done | bytes 8388624 | tf_op jit(solution)/shard_map/all_gather | solution.py:50
  141.8 6.1 %convert_reduce_fusion = (f32[1024]{0:T(1024)S(1)}, f32[1024]{0:T(1024)S(1)}) fusion(bf16[1024,4096]{1,0:T(8,128)(2,1)} %all-gather.2.cloned.1.call-done), kind=kLoop, calls=%fused_computation.4 | loop fusion | flops 16775168 | bytes 8396800 | tf_op jit(solution)/shard_map/reduce_sum | solution.py:52
  147.9 0.0 copy-done.2
  147.9 0.0 copy-done
  147.9 6.8 %fusion.9 = bf16[1024,512]{1,0:T(8,128)(2,1)S(1)} fusion(bf16[4096,512]{1,0:T(8,128)(2,1)} %param.6, bf16[1024,4096]{1,0:T(8,128)(2,1)S(1)} %copy-done, f32[4096]{0:T(1024)S(1)} %copy-done.2, f32[1024]{0:T(1024)S(1)} %get-tuple-element.12, f32[1024]{0:T(1024)S(1)} %get-tuple-element.11), kind=kOutput, calls=%fused_computation.15 | convolution fusion | flops 4316463104 | bytes 13656064 | tf_op jit(solution)/shard_map/dot_general | solution.py:57
  154.8 0.0 copy-start.1
  154.8 0.5 reshape.36
  155.3 0.4 convolution_convert_fusion.1
  155.8 1.5 all_to_all.8
  157.3 14.2 %all-to-all-start = ((bf16[64,2,4096]{2,1,0:T(2,128)(2,1)}), bf16[64,2,4096]{2,1,0:T(2,128)(2,1)S(1)}, u32[]{:S(2)}, u32[]{:S(2)}) async-start(bf16[64,2,4096]{2,1,0:T(2,128)(2,1)} %all_to_all.8), calls=%async_computation | async-start | bytes 2097152 | tf_op jit(solution)/shard_map/all_to_all | solution.py:28
  171.5 30.5 %scatter_custom_fusion = s32[8192]{0:T(1024)S(1)} fusion(s32[8192]{0:T(1024)S(1)} %compare_select_fusion, s32[8192]{0:T(1024)S(1)} %iota.11, s32[]{:T(128)} %constant.54.clone.1), kind=kCustom, calls=%fused_computation.36 | custom fusion | bytes 32772 | tf_op jit(solution)/shard_map/scatter | solution.py:33
  202.0 0.1 and_select_fusion.1
  202.1 0.1 compare_select_fusion.1
  202.2 0.6 gather_fusion
  202.8 0.2 convert_reduce_fusion.2
  203.0 24.5 %all-to-all-done = bf16[64,2,4096]{2,1,0:T(2,128)(2,1)S(1)} async-done(((bf16[64,2,4096]{2,1,0:T(2,128)(2,1)}), bf16[64,2,4096]{2,1,0:T(2,128)(2,1)S(1)}, u32[]{:S(2)}, u32[]{:S(2)}) %all-to-all-start) | async-done | bytes 1048608 | tf_op jit(solution)/shard_map/all_to_all | solution.py:28
  227.5 0.4 all_to_all.10
  227.9 0.5 convolution_convert_fusion
  228.4 1.3 reshape.37
  (9 shorter events, 0.1 us)
Async XLA Ops:
  6.5 141.4 %copy-start.2 = (f32[4096]{0:T(1024)S(1)}, f32[4096]{0:T(1024)}, u32[]{:S(2)}) copy-start(f32[4096]{0:T(1024)} %param.5) | copy-start | bytes 49156
  6.5 135.3 %all-gather.2.cloned.1.call-start = ((), (), s32[]{:S(2)}) async-start(), calls=%async_computation.1 | async-start | bytes 9437184 | tf_op jit(solution)/shard_map/all_gather | solution.py:50
  141.8 6.1 %copy-start = (bf16[1024,4096]{1,0:T(8,128)(2,1)S(1)}, bf16[1024,4096]{1,0:T(8,128)(2,1)}, u32[]{:S(2)}) copy-start(bf16[1024,4096]{1,0:T(8,128)(2,1)} %all-gather.2.cloned.1.call-done) | copy-start | bytes 25165828
  154.8 16.7 %copy-start.1 = (s32[8192]{0:T(1024)S(1)}, s32[8192]{0:T(1024)}, u32[]{:S(2)}) copy-start(s32[8192]{0:T(1024)} %param.7) | copy-start | bytes 98308
  157.3 70.2 %all-to-all-start = ((bf16[64,2,4096]{2,1,0:T(2,128)(2,1)}), bf16[64,2,4096]{2,1,0:T(2,128)(2,1)S(1)}, u32[]{:S(2)}, u32[]{:S(2)}) async-start(bf16[64,2,4096]{2,1,0:T(2,128)(2,1)} %all_to_all.8), calls=%async_computation | async-start | bytes 2097152 | tf_op jit(solution)/shard_map/all_to_all | solution.py:28
Sparse Core Ops, SparseCore 0:
  10.4 131.3 all-gather.1
where the time goes:
time: 237 us
  waiting for transfers between devices  158 us (67%)
  local copies, waits for them, and re-layouts  34.9 us (15%)
  starting transfers between devices  14.2 us (6%)
  between operations  13.5 us (6%)
  other arithmetic  8.2 us (3%)
  matrix products  7.75 us (3%)
    all_gather x1, waiting for transfers between devices, project(): whole_rows = lax.all_gather(memory_rows, 'tp', axis=1, tiled=True)  133 us
    scatter x1, local copies, waits for them, and re-layouts, to_owners(): inverse = jnp.zeros((block_total,), jnp.int32).at[owner_table].set(jnp.ar...  30.5 us
    all_to_all x1, waiting for transfers between devices, to_owners(): lax.all_to_all(outgoing, 'grp', split_axis=0, concat_axis=0, tiled=True)  24.5 us
    all_to_all x1, starting transfers between devices, to_owners(): lax.all_to_all(outgoing, 'grp', split_axis=0, concat_axis=0, tiled=True)  14.2 us
    dot_general x1, matrix products, project(): keys = jnp.dot(normed, key_weight, preferred_element_type=jnp.float32)  6.84 us
    reduce_sum x1, other arithmetic, project(): row_mean = jnp.sum(values, axis=1, keepdims=True) / width  6.09 us
  transfers between devices with their start and end apart: 2, of which 2 were waited for; matrix products, arithmetic and copies ran while one was open for 14% of the time, Pallas kernels for 0%

commit v1 on v0

v1 whole, which is shorter than its diff:
```python
import jax
import jax.numpy as jnp
import numpy as np
from jax import lax
from jax.sharding import Mesh
from jax.sharding import PartitionSpec as P

BLK_ROWS = 8
EPS = 1e-05
TORUS = ("z", "xl", "c", "xh", "y")


def torus_mesh(mesh):
    groups, parts = mesh.devices.shape
    return Mesh(mesh.devices.reshape(groups // 4, 2, 2, 2, parts // 2), TORUS)


def y_ring(step, ring):
    return [
        (core * ring + y, core * ring + (y + (step if core == 0 else -step)) % ring)
        for core in range(2)
        for y in range(ring)
    ]


def crossing():
    return [
        ((xl * 2 + c) * 2 + xh, ((1 - xl) * 2 + c) * 2 + (1 - xh))
        for xl in range(2)
        for c in range(2)
        for xh in range(2)
    ]


def gather_y(piece):
    ring = lax.axis_size("y")
    near = lax.ppermute(piece, ("c", "y"), y_ring(1, ring))
    other = lax.ppermute(piece, ("c", "y"), y_ring(-1, ring))
    far = lax.ppermute(near, ("c", "y"), y_ring(1, ring))
    return [piece, near, other, far]


def piece_owners():
    ring = lax.axis_size("y")
    y = lax.axis_index("y")
    step = 1 - 2 * lax.axis_index("c")
    return [y, (y - step) % ring, (y + step) % ring, (y + 2) % ring]


def half_weights(key_weight, norm_gain):
    xh, core = lax.axis_index("xh"), lax.axis_index("c")
    width, cols = key_weight.shape
    half, quarter, depth = width // 2, width // 4, width // 8
    sent = lax.dynamic_slice(
        key_weight, ((1 - xh) * half + core * quarter, 0), (quarter, cols)
    )
    mine = lax.ppermute(sent, ("xl", "c", "xh"), crossing())
    twin = lax.ppermute(mine, "c", [(0, 1), (1, 0)])
    swapped = jnp.concatenate([mine, twin], axis=0)
    own_parts, other_parts, gain_parts = [], [], []
    for owner in piece_owners():
        start = xh * half + owner * depth
        own_parts.append(lax.dynamic_slice(key_weight, (start, 0), (depth, cols)))
        place = ((owner // 2) ^ core) * 2 + owner % 2
        other_parts.append(lax.dynamic_slice(swapped, (place * depth, 0), (depth, cols)))
        gain_parts.append(lax.dynamic_slice(norm_gain, (start,), (depth,)))
    own = jnp.concatenate(own_parts, axis=0)
    other = jnp.concatenate(other_parts, axis=0)
    first = xh == 0
    weights = jnp.concatenate(
        [jnp.where(first, own, other), jnp.where(first, other, own)], axis=1
    )
    gain = jnp.concatenate(gain_parts)
    gain_sums = jnp.sum(gain[:, None] * weights.astype(jnp.float32), axis=0)
    return weights, gain, gain_sums


def partial_keys(pieces, weights, gain, gain_sums):
    values = jnp.concatenate(pieces, axis=1).astype(jnp.float32)
    half = values.shape[1]
    sums = jnp.sum(values, axis=1)
    squares = jnp.sum(values * values, axis=1)
    here = jnp.stack([sums, squares])
    there = lax.ppermute(here, "xh", [(0, 1), (1, 0)])
    center = sums / half
    scaled = ((values - center[:, None]) * gain[None, :]).astype(jnp.bfloat16)
    product = jnp.dot(scaled, weights, preferred_element_type=jnp.float32)
    both = here + there
    mean = both[0] / (2 * half)
    var = both[1] / (2 * half) - mean * mean
    shifted = product + (center - mean)[:, None] * gain_sums[None, :]
    return (shifted * lax.rsqrt(var + EPS)[:, None]).astype(jnp.bfloat16)


def exchange_x(partial):
    targets, rows, width = partial.shape
    cols = width // 2
    outgoing = partial.reshape(targets, rows, 2, cols).transpose(0, 2, 1, 3)
    outgoing = outgoing.reshape(targets * 2, rows, cols)
    incoming = lax.all_to_all(outgoing, ("xl", "c", "xh"), 0, 0, tiled=True)
    incoming = incoming.reshape(targets, 2, rows, cols).astype(jnp.float32)
    return (incoming[:, 0] + incoming[:, 1]).astype(jnp.bfloat16)


def arrival_slots(owner_table, group, groups, blocks):
    table = owner_table.reshape(groups, blocks)
    ids = jnp.arange(blocks, dtype=jnp.int32)[None, :]
    here = table // blocks == group
    first = jnp.min(jnp.where(here, ids, blocks), axis=1, keepdims=True)
    slots = table % blocks
    slot_a = jnp.sum(jnp.where(ids == first, slots, 0), axis=1)
    slot_b = jnp.sum(jnp.where(here & (ids != first), slots, 0), axis=1)
    return slot_a, slot_b


def on_device(memory_rows, norm_gain, key_weight, owner_table):
    depth_z = lax.axis_size("z")
    groups = 4 * depth_z
    group = (
        lax.axis_index("z") * 4 + lax.axis_index("xl") * 2 + lax.axis_index("c")
    )
    rows, cols = memory_rows.shape
    blocks = rows // BLK_ROWS
    half_rows = rows // 2
    owned = lax.dynamic_slice_in_dim(owner_table, group * blocks, blocks)
    target = owned // blocks
    ids = jnp.arange(blocks, dtype=jnp.int32)
    earlier = (target[None, :] == target[:, None]) & (ids[None, :] < ids[:, None])
    first = jnp.sum(earlier.astype(jnp.int32), axis=1) == 0
    slot = jnp.where(first, target, groups + (target % 4) * depth_z + target // 4)
    sender = (slot[None, :] == ids[:, None]).astype(jnp.bfloat16)
    flattened = memory_rows.reshape(blocks, BLK_ROWS * cols)
    packed = jnp.dot(sender, flattened, preferred_element_type=jnp.float32)
    packed = packed.astype(jnp.bfloat16).reshape(2, half_rows, cols)

    pieces_g = gather_y(packed[1])
    rows_p = lax.all_to_all(
        packed[0].reshape(depth_z, half_rows // depth_z, cols), "z", 0, 0, tiled=True
    )
    weights, gain, gain_sums = half_weights(key_weight, norm_gain)

    partial_g = partial_keys(pieces_g, weights, gain, gain_sums)
    keys_g = exchange_x(partial_g.reshape(4, half_rows // 4, 2 * cols))
    keys_g = keys_g.reshape(4, depth_z, BLK_ROWS, cols).transpose(1, 0, 2, 3)
    keys_g = lax.all_to_all(
        keys_g.reshape(depth_z, 4 * BLK_ROWS, cols), "z", 0, 0, tiled=True
    )

    rows_p = rows_p.reshape(depth_z, 4, BLK_ROWS, cols).transpose(1, 0, 2, 3)
    pieces_p = gather_y(rows_p.reshape(half_rows, cols))
    partial_p = partial_keys(pieces_p, weights, gain, gain_sums)
    keys_p = exchange_x(partial_p.reshape(4, half_rows // 4, 2 * cols))

    slot_a, slot_b = arrival_slots(owner_table, group, groups, blocks)
    slot_a = slot_a.reshape(depth_z, 4).T.reshape(groups)
    slots = jnp.concatenate([slot_a, slot_b])
    picker = (slots[None, :] == ids[:, None]).astype(jnp.bfloat16)
    arrived = jnp.concatenate(
        [
            keys_p.reshape(groups, BLK_ROWS * cols),
            keys_g.reshape(groups, BLK_ROWS * cols),
        ]
    )
    placed = jnp.dot(picker, arrived, preferred_element_type=jnp.float32)
    return placed.astype(jnp.bfloat16).reshape(rows, cols)


def solution(mesh):
    groups, parts = ("z", "xl", "c"), ("xh", "y")
    in_specs = (P(groups, parts), P(), P(None, parts), P())
    return jax.shard_map(
        on_device,
        mesh=torus_mesh(mesh),
        in_specs=in_specs,
        out_specs=P(groups, parts),
        check_vma=False,
    )
```

time: 237 us -> 178 us (0.75)
  the two profiles are of different devices: /device:TPU:2 before, /device:TPU:32 now
where the time goes in v1:
time: 178 us; the launch traced here: 177 us
  waiting for transfers between devices  77.1 us (43%)
  starting transfers between devices  61.9 us (35%)
  local copies, waits for them, and re-layouts  18.1 us (10%)
  matrix products  10.9 us (6%)
  other arithmetic  8.32 us (5%)
    all_to_all x1, waiting for transfers between devices, on_device(): lax.all_to_all(keys_g.reshape(depth_z, 4 * BLK_ROWS, cols), 'z', 0, 0, ti...  28.2 us
    all_to_all x2, waiting for transfers between devices, exchange_x(): incoming = lax.all_to_all(outgoing, ('xl', 'c', 'xh'), 0, 0, tiled=True)  20.6 us
    all_to_all x1, starting transfers between devices, on_device(): lax.all_to_all(packed[0].reshape(depth_z, half_rows // depth_z, cols), 'z...  15.2 us
    dot_general x2, matrix products, partial_keys(): product = jnp.dot(scaled, weights, preferred_element_type=jnp.float32)  10 us
    ppermute x2, waiting for transfers between devices, gather_y(): far = lax.ppermute(near, ('c', 'y'), y_ring(1, ring))  9.82 us
    ppermute x2, starting transfers between devices, gather_y(): other = lax.ppermute(piece, ('c', 'y'), y_ring(-1, ring))  8.69 us
    ppermute x2, waiting for transfers between devices, gather_y(): near = lax.ppermute(piece, ('c', 'y'), y_ring(1, ring))  7.96 us
    all_to_all x1, starting transfers between devices, on_device(): lax.all_to_all(keys_g.reshape(depth_z, 4 * BLK_ROWS, cols), 'z', 0, 0, ti...  7.7 us
  transfers between devices with their start and end apart: 14, of which 9 were waited for; matrix products, arithmetic and copies ran while one was open for 19% of the time, Pallas kernels for 0%

profile of v1, /device:TPU:32, one launch (start us, length us, event | category | flops | bytes accessed | tf_op | source)
XLA Modules:
  0.0 176.9 jit_solution(1826317002493805884)
XLA Ops:
  1.3 4.7 %collective-permute-start.3 = (bf16[1024,512]{1,0:T(8,128)(2,1)S(1)}, bf16[1024,512]{1,0:T(8,128)(2,1)}, u32[]{:S(2)}, u32[]{:S(2)}) collective-permute-start(bf16[1024,512]{1,0:T(8,128)(2,1)S(1)} %constant_dynamic-slice_fusion.4), channel_id=1, source_target_pairs={{0,20},{4,16},{8,28},{12,24},{16,4},{20,0},{24,12},{28,8},{1,21},{... | collective-permute-start | bytes 3145736 | tf_op jit(solution)/shard_map/ppermute | solution.py:57
  10.1 3.5 %collective-permute-start.6 = (bf16[512,512]{1,0:T(8,128)(2,1)S(1)}, bf16[512,512]{1,0:T(8,128)(2,1)S(1)}, u32[]{:S(2)}, u32[]{:S(2)}) collective-permute-start(bf16[512,512]{1,0:T(8,128)(2,1)S(1)} %squeeze.2), channel_id=1, source_target_pairs={{0,1},{1,2},{2,3},{3,0},{8,11},{9,8},{10,9},{11,10},{4,5},{5,6},{6... | collective-permute-start | bytes 1572872 | tf_op jit(solution)/shard_map/ppermute | solution.py:37
  14.6 15.2 %all-to-all-start = ((bf16[16,32,512]{2,1,0:T(8,128)(2,1)}), bf16[16,32,512]{2,1,0:T(8,128)(2,1)S(1)}, u32[]{:S(2)}, u32[]{:S(2)}) async-start(bf16[16,32,512]{2,1,0:T(8,128)(2,1)} %reshape_squeeze.3), calls=%async_computation | async-start | bytes 1048576 | tf_op jit(solution)/shard_map/all_to_all | solution.py:137
  29.8 3.6 %collective-permute-start.7 = (bf16[512,512]{1,0:T(8,128)(2,1)S(1)}, bf16[512,512]{1,0:T(8,128)(2,1)S(1)}, u32[]{:S(2)}, u32[]{:S(2)}) collective-permute-start(bf16[512,512]{1,0:T(8,128)(2,1)S(1)} %squeeze.2), channel_id=1, source_target_pairs={{0,3},{1,0},{2,1},{3,2},{8,9},{9,10},{10,11},{11,8},{4,7},{5,4},{6... | collective-permute-start | bytes 1572872 | tf_op jit(solution)/shard_map/ppermute | solution.py:38
  33.4 2.3 %collective-permute-start.8 = (bf16[512,512]{1,0:T(8,128)(2,1)S(1)}, bf16[512,512]{1,0:T(8,128)(2,1)}, u32[]{:S(2)}, u32[]{:S(2)}) collective-permute-start(bf16[512,512]{1,0:T(8,128)(2,1)S(1)} %collective-permute-done.6), channel_id=1, source_target_pairs={{0,1},{1,2},{2,3},{3,0},{8,11},{9,8},{10,9},{11,10},{4,5},{5,6},{6... | collective-permute-start | bytes 1572872 | tf_op jit(solution)/shard_map/ppermute | solution.py:39
  36.0 2.9 %constant_dynamic-slice_fusion.8 = (bf16[512,512]{1,0:T(8,128)(2,1)}, bf16[512,512]{1,0:T(8,128)(2,1)}, bf16[512,512]{1,0:T(8,128)(2,1)}, bf16[512,512]{1,0:T(8,128)(2,1)}) fusion(bf16[4096,512]{1,0:T(8,128)(2,1)} %param.6, s32[]{:T(128)S(6)} %select_n.139, s32[]{:T(128)S(6)} %select_n.143, s32[]{:T(128)S(6)} %select_n.141, s32[]{:T(128)S(6)} %select_n.145), kind=kLoop, calls=%fused_computation.78 | loop fusion | bytes 4194320 | tf_op jit(solution)/shard_map/dynamic_slice | solution.py:63
  38.9 2.7 %collective-permute-start.4 = (bf16[1024,512]{1,0:T(8,128)(2,1)}, bf16[1024,512]{1,0:T(8,128)(2,1)}, u32[]{:S(2)}, u32[]{:S(2)}) collective-permute-start(bf16[1024,512]{1,0:T(8,128)(2,1)} %collective-permute-done.3), channel_id=1, source_target_pairs={{0,8},{8,0},{1,9},{9,1},{2,10},{10,2},{3,11},{11,3},{4,12},{12,4},... | collective-permute-start | bytes 3145736 | tf_op jit(solution)/shard_map/ppermute | solution.py:58
  41.6 3.8 %collective-permute-done.7 = bf16[512,512]{1,0:T(8,128)(2,1)S(1)} collective-permute-done((bf16[512,512]{1,0:T(8,128)(2,1)S(1)}, bf16[512,512]{1,0:T(8,128)(2,1)S(1)}, u32[]{:S(2)}, u32[]{:S(2)}) %collective-permute-start.7) | collective-permute-done | bytes 524320 | tf_op jit(solution)/shard_map/ppermute | solution.py:38
  48.8 2.7 %collective-permute-start.9 = (f32[2,512]{1,0:T(2,128)S(1)}, f32[2,512]{1,0:T(2,128)S(1)}, u32[]{:S(2)}, u32[]{:S(2)}) collective-permute-start(f32[2,512]{1,0:T(2,128)S(1)} %pad_maximum_fusion.9), channel_id=1, source_target_pairs={{0,4},{4,0},{1,5},{5,1},{2,6},{6,2},{3,7},{7,3},{8,12},{12,8},{9,1... | collective-permute-start | bytes 12296 | tf_op jit(solution)/shard_map/ppermute | solution.py:84
  52.8 3.0 %collective-permute-done.9 = f32[2,512]{1,0:T(2,128)S(1)} collective-permute-done((f32[2,512]{1,0:T(2,128)S(1)}, f32[2,512]{1,0:T(2,128)S(1)}, u32[]{:S(2)}, u32[]{:S(2)}) %collective-permute-start.9) | collective-permute-done | bytes 4128 | tf_op jit(solution)/shard_map/ppermute | solution.py:84
  55.8 3.7 %all-to-all-done = bf16[16,32,512]{2,1,0:T(8,128)(2,1)S(1)} async-done(((bf16[16,32,512]{2,1,0:T(8,128)(2,1)}), bf16[16,32,512]{2,1,0:T(8,128)(2,1)S(1)}, u32[]{:S(2)}, u32[]{:S(2)}) %all-to-all-start) | async-done | bytes 524320 | tf_op jit(solution)/shard_map/all_to_all | solution.py:137
  61.7 5.1 %collective-permute-start.1 = (bf16[512,512]{1,0:T(8,128)(2,1)S(1)}, bf16[512,512]{1,0:T(8,128)(2,1)S(1)}, u32[]{:S(2)}, u32[]{:S(2)}) collective-permute-start(bf16[512,512]{1,0:T(8,128)(2,1)S(1)} %bitcast.88), channel_id=1, source_target_pairs={{0,3},{1,0},{2,1},{3,2},{8,9},{9,10},{10,11},{11,8},{4,7},{5,4},{6... | collective-permute-start | bytes 1572872 | tf_op jit(solution)/shard_map/ppermute | solution.py:38
  68.3 8.0 %collective-permute-done = bf16[512,512]{1,0:T(8,128)(2,1)S(1)} collective-permute-done((bf16[512,512]{1,0:T(8,128)(2,1)S(1)}, bf16[512,512]{1,0:T(8,128)(2,1)S(1)}, u32[]{:S(2)}, u32[]{:S(2)}) %collective-permute-start) | collective-permute-done | bytes 524320 | tf_op jit(solution)/shard_map/ppermute | solution.py:37
  76.3 2.1 %collective-permute-start.2 = (bf16[512,512]{1,0:T(8,128)(2,1)S(1)}, bf16[512,512]{1,0:T(8,128)(2,1)S(1)}, u32[]{:S(2)}, u32[]{:S(2)}) collective-permute-start(bf16[512,512]{1,0:T(8,128)(2,1)S(1)} %collective-permute-done), channel_id=1, source_target_pairs={{0,1},{1,2},{2,3},{3,0},{8,11},{9,8},{10,9},{11,10},{4,5},{5,6},{6... | collective-permute-start | bytes 1572872 | tf_op jit(solution)/shard_map/ppermute | solution.py:39
  80.4 8.2 %collective-permute-done.2 = bf16[512,512]{1,0:T(8,128)(2,1)S(1)} collective-permute-done((bf16[512,512]{1,0:T(8,128)(2,1)S(1)}, bf16[512,512]{1,0:T(8,128)(2,1)S(1)}, u32[]{:S(2)}, u32[]{:S(2)}) %collective-permute-start.2) | collective-permute-done | bytes 524320 | tf_op jit(solution)/shard_map/ppermute | solution.py:39
  89.3 2.7 %collective-permute-start.5 = (f32[2,512]{1,0:T(2,128)S(1)}, f32[2,512]{1,0:T(2,128)S(1)}, u32[]{:S(2)}, u32[]{:S(2)}) collective-permute-start(f32[2,512]{1,0:T(2,128)S(1)} %pad_maximum_fusion.8), channel_id=1, source_target_pairs={{0,4},{4,0},{1,5},{5,1},{2,6},{6,2},{3,7},{7,3},{8,12},{12,8},{9,1... | collective-permute-start | bytes 12296 | tf_op jit(solution)/shard_map/ppermute | solution.py:84
  92.1 4.4 %multiply_convert_fusion = bf16[512,1024]{1,0:T(8,128)(2,1)} fusion(f32[512]{0:T(512)S(1)} %get-tuple-element.35, f32[2048]{0:T(1024)S(1)} %pad_maximum_fusion.7, bf16[2048,512]{1,0:T(8,128)(2,1)S(1)} %get-tuple-element.12, bf16[2048,512]{1,0:T(8,128)(2,1)S(1)} %get-tuple-element.11, f32[512]{0:T(512)S(1)} %get-tuple-element.36, ...), kind=kOutput, calls=%fused_computation.22 | convolution fusion | flops 2169503744 | bytes 7358464 | tf_op jit(solution)/shard_map/dot_general | solution.py:87
  99.5 4.0 %all-to-all-start.2 = ((bf16[8,128,512]{2,1,0:T(8,128)(2,1)}), bf16[8,128,512]{2,1,0:T(8,128)(2,1)S(1)}, u32[]{:S(2)}, u32[]{:S(2)}) async-start(bf16[8,128,512]{2,1,0:T(8,128)(2,1)} %bitcast.85), calls=%async_computation.2 | async-start | bytes 2097152 | tf_op jit(solution)/shard_map/all_to_all | solution.py:100
  103.6 5.6 %multiply_convert_fusion.1 = bf16[512,1024]{1,0:T(8,128)(2,1)} fusion(f32[2048]{0:T(1024)S(1)} %pad_maximum_fusion.7, f32[512]{0:T(512)S(1)} %get-tuple-element.32, bf16[2048,512]{1,0:T(8,128)(2,1)} %copy-done, bf16[2048,512]{1,0:T(8,128)(2,1)S(1)} %get-tuple-element.11, f32[512]{0:T(512)S(1)} %get-tuple-element.33, f32[1024]{0:T(1024)S(1)} %multiply_reduce_fusion, ...), kind=kOutput, calls=%fused_computation.24 | convolution fusion | flops 2169503744 | bytes 7358464 | tf_op jit(solution)/shard_map/dot_general | solution.py:87
  112.2 6.6 %all-to-all-done.2 = bf16[8,128,512]{2,1,0:T(8,128)(2,1)S(1)} async-done(((bf16[8,128,512]{2,1,0:T(8,128)(2,1)}), bf16[8,128,512]{2,1,0:T(8,128)(2,1)S(1)}, u32[]{:S(2)}, u32[]{:S(2)}) %all-to-all-start.2) | async-done | bytes 1048608 | tf_op jit(solution)/shard_map/all_to_all | solution.py:100
  118.8 3.7 %all-to-all-start.1 = ((bf16[8,128,512]{2,1,0:T(8,128)(2,1)}), bf16[8,128,512]{2,1,0:T(8,128)(2,1)S(1)}, u32[]{:S(2)}, u32[]{:S(2)}) async-start(bf16[8,128,512]{2,1,0:T(8,128)(2,1)} %bitcast.11), calls=%async_computation.1 | async-start | bytes 2097152 | tf_op jit(solution)/shard_map/all_to_all | solution.py:100
  123.7 14.0 %all-to-all-done.1 = bf16[8,128,512]{2,1,0:T(8,128)(2,1)S(1)} async-done(((bf16[8,128,512]{2,1,0:T(8,128)(2,1)}), bf16[8,128,512]{2,1,0:T(8,128)(2,1)S(1)}, u32[]{:S(2)}, u32[]{:S(2)}) %all-to-all-start.1) | async-done | bytes 1048608 | tf_op jit(solution)/shard_map/all_to_all | solution.py:100
  137.7 7.7 %all-to-all-start.3 = ((bf16[16,32,512]{2,1,0:T(8,128)(2,1)}), bf16[16,32,512]{2,1,0:T(8,128)(2,1)S(1)}, u32[]{:S(2)}, u32[]{:S(2)}) async-start(bf16[16,32,512]{2,1,0:T(8,128)(2,1)} %copy_bitcast_fusion), calls=%async_computation.3 | async-start | bytes 1048576 | tf_op jit(solution)/shard_map/all_to_all | solution.py:145
  146.8 28.2 %all-to-all-done.3 = bf16[16,32,512]{2,1,0:T(8,128)(2,1)S(1)} async-done(((bf16[16,32,512]{2,1,0:T(8,128)(2,1)}), bf16[16,32,512]{2,1,0:T(8,128)(2,1)S(1)}, u32[]{:S(2)}, u32[]{:S(2)}) %all-to-all-start.3) | async-done | bytes 524320 | tf_op jit(solution)/shard_map/all_to_all | solution.py:145
  (82 shorter events, 28.1 us)
Async XLA Ops:
  1.3 37.6 %collective-permute-start.3 = (bf16[1024,512]{1,0:T(8,128)(2,1)S(1)}, bf16[1024,512]{1,0:T(8,128)(2,1)}, u32[]{:S(2)}, u32[]{:S(2)}) collective-permute-start(bf16[1024,512]{1,0:T(8,128)(2,1)S(1)} %constant_dynamic-slice_fusion.4), channel_id=1, source_target_pairs={{0,20},{4,16},{8,28},{12,24},{16,4},{20,0},{24,12},{28,8},{1,21},{... | collective-permute-start | bytes 3145736 | tf_op jit(solution)/shard_map/ppermute | solution.py:57
  9.3 26.6 %copy-start.14 = (f32[4096]{0:T(1024)S(1)}, f32[4096]{0:T(1024)}, u32[]{:S(2)}) copy-start(f32[4096]{0:T(1024)} %param.5) | copy-start | bytes 49156
  10.1 23.3 %collective-permute-start.6 = (bf16[512,512]{1,0:T(8,128)(2,1)S(1)}, bf16[512,512]{1,0:T(8,128)(2,1)S(1)}, u32[]{:S(2)}, u32[]{:S(2)}) collective-permute-start(bf16[512,512]{1,0:T(8,128)(2,1)S(1)} %squeeze.2), channel_id=1, source_target_pairs={{0,1},{1,2},{2,3},{3,0},{8,11},{9,8},{10,9},{11,10},{4,5},{5,6},{6... | collective-permute-start | bytes 1572872 | tf_op jit(solution)/shard_map/ppermute | solution.py:37
  14.6 44.9 %all-to-all-start = ((bf16[16,32,512]{2,1,0:T(8,128)(2,1)}), bf16[16,32,512]{2,1,0:T(8,128)(2,1)S(1)}, u32[]{:S(2)}, u32[]{:S(2)}) async-start(bf16[16,32,512]{2,1,0:T(8,128)(2,1)} %reshape_squeeze.3), calls=%async_computation | async-start | bytes 1048576 | tf_op jit(solution)/shard_map/all_to_all | solution.py:137
  29.8 15.5 %collective-permute-start.7 = (bf16[512,512]{1,0:T(8,128)(2,1)S(1)}, bf16[512,512]{1,0:T(8,128)(2,1)S(1)}, u32[]{:S(2)}, u32[]{:S(2)}) collective-permute-start(bf16[512,512]{1,0:T(8,128)(2,1)S(1)} %squeeze.2), channel_id=1, source_target_pairs={{0,3},{1,0},{2,1},{3,2},{8,9},{9,10},{10,11},{11,8},{4,7},{5,4},{6... | collective-permute-start | bytes 1572872 | tf_op jit(solution)/shard_map/ppermute | solution.py:38
  33.4 15.4 %copy-start.6 = (bf16[512,512]{1,0:T(8,128)(2,1)}, bf16[512,512]{1,0:T(8,128)(2,1)S(1)}, u32[]{:S(2)}) copy-start(bf16[512,512]{1,0:T(8,128)(2,1)S(1)} %collective-permute-done.6) | copy-start | bytes 1572868
  33.4 13.6 %collective-permute-start.8 = (bf16[512,512]{1,0:T(8,128)(2,1)S(1)}, bf16[512,512]{1,0:T(8,128)(2,1)}, u32[]{:S(2)}, u32[]{:S(2)}) collective-permute-start(bf16[512,512]{1,0:T(8,128)(2,1)S(1)} %collective-permute-done.6), channel_id=1, source_target_pairs={{0,1},{1,2},{2,3},{3,0},{8,11},{9,8},{10,9},{11,10},{4,5},{5,6},{6... | collective-permute-start | bytes 1572872 | tf_op jit(solution)/shard_map/ppermute | solution.py:39
  38.9 28.0 %collective-permute-start.4 = (bf16[1024,512]{1,0:T(8,128)(2,1)}, bf16[1024,512]{1,0:T(8,128)(2,1)}, u32[]{:S(2)}, u32[]{:S(2)}) collective-permute-start(bf16[1024,512]{1,0:T(8,128)(2,1)} %collective-permute-done.3), channel_id=1, source_target_pairs={{0,8},{8,0},{1,9},{9,1},{2,10},{10,2},{3,11},{11,3},{4,12},{12,4},... | collective-permute-start | bytes 3145736 | tf_op jit(solution)/shard_map/ppermute | solution.py:58
  48.8 7.0 %collective-permute-start.9 = (f32[2,512]{1,0:T(2,128)S(1)}, f32[2,512]{1,0:T(2,128)S(1)}, u32[]{:S(2)}, u32[]{:S(2)}) collective-permute-start(f32[2,512]{1,0:T(2,128)S(1)} %pad_maximum_fusion.9), channel_id=1, source_target_pairs={{0,4},{4,0},{1,5},{5,1},{2,6},{6,2},{3,7},{7,3},{8,12},{12,8},{9,1... | collective-permute-start | bytes 12296 | tf_op jit(solution)/shard_map/ppermute | solution.py:84
  59.5 18.8 %copy-start.2 = (bf16[512,512]{1,0:T(8,128)(2,1)S(1)}, bf16[512,512]{1,0:T(8,128)(2,1)}, u32[]{:S(2)}) copy-start(bf16[512,512]{1,0:T(8,128)(2,1)} %get-tuple-element.13) | copy-start | bytes 1572868
  59.5 18.8 %copy-start.3 = (bf16[512,512]{1,0:T(8,128)(2,1)S(1)}, bf16[512,512]{1,0:T(8,128)(2,1)}, u32[]{:S(2)}) copy-start(bf16[512,512]{1,0:T(8,128)(2,1)} %get-tuple-element.14) | copy-start | bytes 1572868
  59.5 18.8 %copy-start.4 = (bf16[512,512]{1,0:T(8,128)(2,1)S(1)}, bf16[512,512]{1,0:T(8,128)(2,1)}, u32[]{:S(2)}) copy-start(bf16[512,512]{1,0:T(8,128)(2,1)} %get-tuple-element.15) | copy-start | bytes 1572868
  59.6 18.8 %copy-start.5 = (bf16[512,512]{1,0:T(8,128)(2,1)S(1)}, bf16[512,512]{1,0:T(8,128)(2,1)}, u32[]{:S(2)}) copy-start(bf16[512,512]{1,0:T(8,128)(2,1)} %get-tuple-element.16) | copy-start | bytes 1572868
  59.6 28.9 %copy-start.1 = (bf16[16,4,8,512]{3,2,0,1:T(8,128)(2,1)}, bf16[16,4,8,512]{3,2,0,1:T(8,128)(2,1)S(1)}, u32[]{:S(2)}) copy-start(bf16[16,4,8,512]{3,2,0,1:T(8,128)(2,1)S(1)} %copy.21) | copy-start | bytes 1572868
  59.6 16.6 %collective-permute-start = (bf16[512,512]{1,0:T(8,128)(2,1)S(1)}, bf16[512,512]{1,0:T(8,128)(2,1)S(1)}, u32[]{:S(2)}, u32[]{:S(2)}) collective-permute-start(bf16[512,512]{1,0:T(8,128)(2,1)S(1)} %bitcast.87), channel_id=1, source_target_pairs={{0,1},{1,2},{2,3},{3,0},{8,11},{9,8},{10,9},{11,10},{4,5},{5,6},{6... | collective-permute-start | bytes 1572872 | tf_op jit(solution)/shard_map/ppermute | solution.py:37
  61.7 18.6 %collective-permute-start.1 = (bf16[512,512]{1,0:T(8,128)(2,1)S(1)}, bf16[512,512]{1,0:T(8,128)(2,1)S(1)}, u32[]{:S(2)}, u32[]{:S(2)}) collective-permute-start(bf16[512,512]{1,0:T(8,128)(2,1)S(1)} %bitcast.88), channel_id=1, source_target_pairs={{0,3},{1,0},{2,1},{3,2},{8,9},{9,10},{10,11},{11,8},{4,7},{5,4},{6... | collective-permute-start | bytes 1572872 | tf_op jit(solution)/shard_map/ppermute | solution.py:38
  76.3 12.3 %collective-permute-start.2 = (bf16[512,512]{1,0:T(8,128)(2,1)S(1)}, bf16[512,512]{1,0:T(8,128)(2,1)S(1)}, u32[]{:S(2)}, u32[]{:S(2)}) collective-permute-start(bf16[512,512]{1,0:T(8,128)(2,1)S(1)} %collective-permute-done), channel_id=1, source_target_pairs={{0,1},{1,2},{2,3},{3,0},{8,11},{9,8},{10,9},{11,10},{4,5},{5,6},{6... | collective-permute-start | bytes 1572872 | tf_op jit(solution)/shard_map/ppermute | solution.py:39
  79.3 12.8 %copy-start.7 = (bf16[512,512]{1,0:T(8,128)(2,1)S(1)}, bf16[512,512]{1,0:T(8,128)(2,1)}, u32[]{:S(2)}) copy-start(bf16[512,512]{1,0:T(8,128)(2,1)} %copy-done.6) | copy-start | bytes 1572868
  79.3 12.8 %copy-start.9 = (bf16[512,512]{1,0:T(8,128)(2,1)S(1)}, bf16[512,512]{1,0:T(8,128)(2,1)}, u32[]{:S(2)}) copy-start(bf16[512,512]{1,0:T(8,128)(2,1)} %copy-done.8) | copy-start | bytes 1572868
  89.3 14.2 %collective-permute-start.5 = (f32[2,512]{1,0:T(2,128)S(1)}, f32[2,512]{1,0:T(2,128)S(1)}, u32[]{:S(2)}, u32[]{:S(2)}) collective-permute-start(f32[2,512]{1,0:T(2,128)S(1)} %pad_maximum_fusion.8), channel_id=1, source_target_pairs={{0,4},{4,0},{1,5},{5,1},{2,6},{6,2},{3,7},{7,3},{8,12},{12,8},{9,1... | collective-permute-start | bytes 12296 | tf_op jit(solution)/shard_map/ppermute | solution.py:84
  99.5 19.3 %all-to-all-start.2 = ((bf16[8,128,512]{2,1,0:T(8,128)(2,1)}), bf16[8,128,512]{2,1,0:T(8,128)(2,1)S(1)}, u32[]{:S(2)}, u32[]{:S(2)}) async-start(bf16[8,128,512]{2,1,0:T(8,128)(2,1)} %bitcast.85), calls=%async_computation.2 | async-start | bytes 2097152 | tf_op jit(solution)/shard_map/all_to_all | solution.py:100
  118.8 26.6 %copy-start.13 = (s32[8192]{0:T(1024)S(1)}, s32[8192]{0:T(1024)}, u32[]{:S(2)}) copy-start(s32[8192]{0:T(1024)} %param.7) | copy-start | bytes 98308
  118.8 18.9 %all-to-all-start.1 = ((bf16[8,128,512]{2,1,0:T(8,128)(2,1)}), bf16[8,128,512]{2,1,0:T(8,128)(2,1)S(1)}, u32[]{:S(2)}, u32[]{:S(2)}) async-start(bf16[8,128,512]{2,1,0:T(8,128)(2,1)} %bitcast.11), calls=%async_computation.1 | async-start | bytes 2097152 | tf_op jit(solution)/shard_map/all_to_all | solution.py:100
  137.7 37.3 %all-to-all-start.3 = ((bf16[16,32,512]{2,1,0:T(8,128)(2,1)}), bf16[16,32,512]{2,1,0:T(8,128)(2,1)S(1)}, u32[]{:S(2)}, u32[]{:S(2)}) async-start(bf16[16,32,512]{2,1,0:T(8,128)(2,1)} %copy_bitcast_fusion), calls=%async_computation.3 | async-start | bytes 1048576 | tf_op jit(solution)/shard_map/all_to_all | solution.py:145
  (5 other events, 43.7 us)

commit v2 on v0

v2 whole, which is shorter than its diff:
```python
import functools

import jax
import jax.numpy as jnp
from jax import lax
from jax.experimental import pallas as pl
from jax.experimental.pallas import tpu as pltpu
from jax.sharding import Mesh
from jax.sharding import PartitionSpec as P

BLK = 8
EPS = 1e-05
TORUS = ("z", "xl", "c", "xh", "y")
SUBCUBE = ("xl", "c", "xh")
VMEM = pl.BlockSpec(memory_space=pltpu.VMEM)
SMEM = pl.BlockSpec(memory_space=pltpu.SMEM)
F32, BF16 = jnp.float32, jnp.bfloat16


def torus_mesh(mesh):
    groups, parts = mesh.devices.shape
    return Mesh(mesh.devices.reshape(groups // 4, 2, 2, 2, parts // 2), TORUS)


def y_ring(step, ring):
    return [
        (core * ring + y, core * ring + (y + (step if core == 0 else -step)) % ring)
        for core in range(2)
        for y in range(ring)
    ]


def crossing():
    return [
        ((xl * 2 + c) * 2 + xh, ((1 - xl) * 2 + c) * 2 + (1 - xh))
        for xl in range(2)
        for c in range(2)
        for xh in range(2)
    ]


def gather_y(piece):
    ring = lax.axis_size("y")
    near = lax.ppermute(piece, ("c", "y"), y_ring(1, ring))
    other = lax.ppermute(piece, ("c", "y"), y_ring(-1, ring))
    far = lax.ppermute(near, ("c", "y"), y_ring(1, ring))
    return [piece, near, other, far]


def pack_kernel(groups, owned, rows, first, second, count):
    blocks = rows.shape[0]
    shift = blocks.bit_length() - 1

    def clear(i, carry):
        count[i] = 0
        return carry

    def place(b, carry):
        target = owned[b] >> shift
        seen = count[target]
        count[target] = seen + 1

        @pl.when(seen == 0)
        def _():
            first[target] = rows[b]

        @pl.when(seen != 0)
        def _():
            second[target] = rows[b]

        return carry

    lax.fori_loop(0, groups, clear, 0, unroll=8)
    lax.fori_loop(0, blocks, place, 0, unroll=4)


def pack(memory_rows, owned, groups):
    rows, cols = memory_rows.shape
    blocks = rows // BLK
    out = jax.ShapeDtypeStruct((groups, BLK, cols), BF16)
    return pl.pallas_call(
        functools.partial(pack_kernel, groups),
        out_shape=(out, out),
        in_specs=[SMEM, VMEM],
        out_specs=(VMEM, VMEM),
        scratch_shapes=[pltpu.SMEM((groups,), jnp.int32)],
        cost_estimate=pl.CostEstimate(flops=1 << 20, bytes_accessed=4 * rows * cols, transcendentals=0),
        name="pack",
    )(owned, memory_rows.reshape(blocks, BLK, cols))


def two_parts(value):
    high = value.astype(BF16).astype(F32)
    return high, value - high


def key_kernel(where, p0, p1, p2, p3, gain, w_own, w_mine, w_twin, kept, table, sent, scaled, acc):
    step = pl.program_id(0)
    parts = (p0, p1, p2, p3)
    rows, width = p0.shape
    half = width * 4
    tile = 128
    tiles = rows // BLK

    @pl.when(step == 0)
    def _():
        sent[tiles] = jnp.zeros(sent.shape[1:], BF16)
        for q in range(rows // tile):
            here = pl.ds(q * tile, tile)
            total = jnp.zeros((tile, 1), F32)
            square = jnp.zeros((tile, 1), F32)
            for part in parts:
                v = part[here, :].astype(F32)
                total += jnp.sum(v, axis=1, keepdims=True)
                square += jnp.sum(v * v, axis=1, keepdims=True)
            mean = total / half
            center, rest = two_parts(mean)
            high, low = two_parts(square / half - mean * mean)
            for j, part in enumerate(parts):
                v = part[here, :].astype(F32)
                scaled[j, here, :] = ((v - center) * gain[j]).astype(BF16)
            lane = lax.broadcasted_iota(jnp.int32, (tile, 128), 1)
            stats = jnp.where(lane == 0, center, 0.0)
            stats = jnp.where(lane == 1, rest, stats)
            stats = jnp.where(lane == 2, high, stats)
            stats = jnp.where(lane == 3, low, stats)
            table[here, :] = stats
            sent[tiles, :, q * 128 : (q + 1) * 128] = jnp.transpose(stats)[0:BLK, :].astype(BF16)

    left = scaled[step]
    from_mine = where[4 + step] < 2
    own = jnp.dot(left, w_own[...], preferred_element_type=F32)

    @pl.when(step == 0)
    def _():
        kept[...] = own
        acc[...] = jnp.zeros_like(own)

    @pl.when(step != 0)
    def _():
        kept[...] += own

    @pl.when(from_mine)
    def _():
        acc[...] += jnp.dot(left, w_mine[...], preferred_element_type=F32)

    @pl.when(jnp.logical_not(from_mine))
    def _():
        acc[...] += jnp.dot(left, w_twin[...], preferred_element_type=F32)

    @pl.when(step == 3)
    def _():
        sent[0:tiles] = acc[...].reshape(tiles, BLK, acc.shape[1]).astype(BF16)


def project(pieces, where, gain, key_weight, mine, twin):
    rows, width = pieces[0].shape
    tiles = rows // BLK
    cols = key_weight.shape[1]
    whole = pl.BlockSpec((rows, width), lambda j, s: (0, 0))
    return pl.pallas_call(
        key_kernel,
        out_shape=(
            jax.ShapeDtypeStruct((rows, cols), F32),
            jax.ShapeDtypeStruct((rows, 128), F32),
            jax.ShapeDtypeStruct((tiles + 1, BLK, cols), BF16),
        ),
        grid_spec=pltpu.PrefetchScalarGridSpec(
            num_scalar_prefetch=1,
            grid=(4,),
            in_specs=[whole] * 4
            + [
                pl.BlockSpec((4, 1, width), lambda j, s: (0, 0, 0)),
                pl.BlockSpec((width, cols), lambda j, s: (s[j], 0)),
                pl.BlockSpec((width, cols), lambda j, s: (s[4 + j] & 1, 0)),
                pl.BlockSpec((width, cols), lambda j, s: (s[4 + j] & 1, 0)),
            ],
            out_specs=(
                pl.BlockSpec((rows, cols), lambda j, s: (0, 0)),
                pl.BlockSpec((rows, 128), lambda j, s: (0, 0)),
                pl.BlockSpec((tiles + 1, BLK, cols), lambda j, s: (0, 0, 0)),
            ),
            scratch_shapes=[
                pltpu.VMEM((4, rows, width), BF16),
                pltpu.VMEM((rows, cols), F32),
            ],
        ),
        cost_estimate=pl.CostEstimate(
            flops=2 * rows * width * 4 * cols * 2, bytes_accessed=8 << 20, transcendentals=0
        ),
    )(where, *pieces, gain, key_weight, mine, twin)


def whole_keys(kept, table, came, gain_sums, q):
    tiles = came.shape[0] - 1
    cols = came.shape[2]
    here = pl.ds(q * 128, 128)
    per = 128 // BLK
    value_b = came[q * per : (q + 1) * per].astype(F32).reshape(128, cols)
    stats = came[tiles, :, q * 128 : (q + 1) * 128].astype(F32)
    stats = jnp.concatenate([stats, jnp.zeros((128 - BLK, 128), F32)], axis=0)
    stats_b = jnp.transpose(stats)
    stats_a = table[here, :]
    center_a, center_b = stats_a[:, 0:1], stats_b[:, 0:1]
    mean_a, mean_b = center_a + stats_a[:, 1:2], center_b + stats_b[:, 1:2]
    var_a, var_b = stats_a[:, 2:3] + stats_a[:, 3:4], stats_b[:, 2:3] + stats_b[:, 3:4]
    mean = 0.5 * (mean_a + mean_b)
    gap = 0.5 * (mean_a - mean_b)
    scale = lax.rsqrt(0.5 * (var_a + var_b) + gap * gap + EPS)
    shift = (center_a - mean) * gain_sums[0:1, :] + (center_b - mean) * gain_sums[1:2, :]
    keys = (kept[here, :] + value_b + shift) * scale
    return keys.reshape(per, BLK, cols).astype(BF16)


def sum_kernel(kept, table, came, gain_sums, out):
    per = 128 // BLK
    for q in range(kept.shape[0] // 128):
        out[q * per : (q + 1) * per] = whole_keys(kept, table, came, gain_sums, q)


def sum_partials(kept, table, came, gain_sums):
    tiles, _, cols = came.shape
    return pl.pallas_call(
        sum_kernel,
        out_shape=jax.ShapeDtypeStruct((tiles - 1, BLK, cols), BF16),
        in_specs=[VMEM] * 4,
        out_specs=VMEM,
        cost_estimate=pl.CostEstimate(flops=1 << 22, bytes_accessed=4 << 20, transcendentals=0),
        name="sum_g",
    )(kept, table, came, gain_sums)


def place_kernel(slots, kept, table, came, gain_sums, others, out):
    groups = others.shape[0]
    per = 128 // BLK
    for q in range(kept.shape[0] // 128):
        keys = whole_keys(kept, table, came, gain_sums, q)
        for i in range(per):
            out[slots[q * per + i]] = keys[i]

    def put(i, carry):
        out[slots[groups + i]] = others[i]
        return carry

    lax.fori_loop(0, groups, put, 0, unroll=8)


def place(slots, kept, table, came, gain_sums, others):
    _, _, cols = came.shape
    blocks = slots.shape[0]
    return pl.pallas_call(
        place_kernel,
        out_shape=jax.ShapeDtypeStruct((blocks, BLK, cols), BF16),
        in_specs=[SMEM] + [VMEM] * 5,
        out_specs=VMEM,
        cost_estimate=pl.CostEstimate(flops=1 << 22, bytes_accessed=4 << 20, transcendentals=0),
        name="place",
    )(slots, kept, table, came, gain_sums, others)


def arrival_slots(owner_table, group, groups, blocks):
    table = owner_table.reshape(groups, blocks)
    ids = jnp.arange(blocks, dtype=jnp.int32)[None, :]
    here = table // blocks == group
    first = jnp.min(jnp.where(here, ids, blocks), axis=1, keepdims=True)
    slots = table % blocks
    slot_a = jnp.sum(jnp.where(ids == first, slots, 0), axis=1)
    slot_b = jnp.sum(jnp.where(here & (ids != first), slots, 0), axis=1)
    return jnp.concatenate([slot_a, slot_b])


def steps(memory_rows, norm_gain, key_weight, owner_table):
    depth_z = lax.axis_size("z")
    ring = lax.axis_size("y")
    groups = 4 * depth_z
    xh, core, y = lax.axis_index("xh"), lax.axis_index("c"), lax.axis_index("y")
    group = lax.axis_index("z") * 4 + lax.axis_index("xl") * 2 + core
    rows, cols = memory_rows.shape
    blocks, half_rows = rows // BLK, rows // 2
    width, outs = key_weight.shape

    sent = lax.dynamic_slice(
        key_weight,
        ((1 - xh) * (width // 2) + core * (width // 4), 0),
        (width // 4, outs),
    )
    mine = lax.ppermute(sent, SUBCUBE, crossing())
    twin = lax.ppermute(mine, "c", [(0, 1), (1, 0)])

    owned = lax.dynamic_slice_in_dim(owner_table, group * blocks, blocks)
    packed_p, packed_g = pack(memory_rows, owned, groups)
    pieces_g = gather_y(packed_g.reshape(half_rows, cols))
    rows_p = lax.all_to_all(packed_p, ("z", "xl", "c"), 0, 0, tiled=True)

    step = 1 - 2 * core
    owners = jnp.stack([y, (y - step) % ring, (y + step) % ring, (y + 2) % ring])
    places = ((owners // 2) ^ core) * 2 + owners % 2
    where = jnp.concatenate([xh * 4 + owners, places, xh[None]]).astype(jnp.int32)
    gain = norm_gain.reshape(8, 1, cols)[xh * 4 + owners]
    gain_sums = jnp.sum(
        (norm_gain[:, None] * key_weight.astype(F32)).reshape(2, width // 2, outs), axis=1
    )
    gain_sums = jnp.where(xh == 0, gain_sums, gain_sums[::-1])
    slots = arrival_slots(owner_table, group, groups, blocks)

    pair = [(0, 1), (1, 0)]
    kept_g, table_g, sent_g = project(pieces_g, where, gain, key_weight, mine, twin)
    came_g = lax.ppermute(sent_g, "xh", pair)
    keys_g = sum_partials(kept_g, table_g, came_g, gain_sums)
    keys_g = lax.all_to_all(keys_g, ("z", "xl", "c"), 0, 0, tiled=True)

    pieces_p = gather_y(rows_p.reshape(half_rows, cols))
    kept_p, table_p, sent_p = project(pieces_p, where, gain, key_weight, mine, twin)
    came_p = lax.ppermute(sent_p, "xh", pair)
    placed = place(slots, kept_p, table_p, came_p, gain_sums, keys_g)
    return placed.reshape(rows, outs)


def solution(mesh):
    groups, parts = ("z", "xl", "c"), ("xh", "y")
    torus = torus_mesh(mesh)
    return jax.shard_map(
        steps,
        mesh=torus,
        in_specs=(P(groups, parts), P(), P(None, parts), P()),
        out_specs=P(groups, parts),
        check_vma=False,
    )
```

time: 237 us -> 156 us (0.66)
  the two profiles are of different devices: /device:TPU:2 before, /device:TPU:26 now
where the time goes in v2:
time: 156 us
  starting transfers between devices  57.9 us (37%)
  waiting for transfers between devices  54.2 us (35%)
  Pallas kernels  30.7 us (20%)
  local copies, waits for them, and re-layouts  7.46 us (5%)
  other arithmetic  5 us (3%)
    pallas_call x2, Pallas kernels, project(): pl.pallas_call(key_kernel, out_shape=(jax.ShapeDtypeStruct((rows, cols),...  19.3 us
    all_to_all x1, starting transfers between devices, steps(): rows_p = lax.all_to_all(packed_p, ('z', 'xl', 'c'), 0, 0, tiled=True)  17.4 us
    ppermute x2, waiting for transfers between devices, gather_y(): far = lax.ppermute(near, ('c', 'y'), y_ring(1, ring))  16.1 us
    ppermute x2, waiting for transfers between devices, gather_y(): near = lax.ppermute(piece, ('c', 'y'), y_ring(1, ring))  15 us
    all_to_all x1, starting transfers between devices, steps(): keys_g = lax.all_to_all(keys_g, ('z', 'xl', 'c'), 0, 0, tiled=True)  13.6 us
    ppermute x1, waiting for transfers between devices, steps(): came_p = lax.ppermute(sent_p, 'xh', pair)  11.6 us
    ppermute x1, waiting for transfers between devices, steps(): came_g = lax.ppermute(sent_g, 'xh', pair)  11.1 us
    ppermute x2, starting transfers between devices, gather_y(): other = lax.ppermute(piece, ('c', 'y'), y_ring(-1, ring))  6.9 us
  transfers between devices with their start and end apart: 12, of which 7 were waited for; matrix products, arithmetic and copies ran while one was open for 5% of the time, Pallas kernels for 17%

profile of v2, /device:TPU:26, one launch (start us, length us, event | category | flops | bytes accessed | tf_op | source)
XLA Modules:
  0.0 155.6 jit_solution(11825779081090286507)
XLA Ops:
  1.3 3.4 %collective-permute-start.3 = (bf16[1024,512]{1,0:T(8,128)(2,1)S(1)}, bf16[1024,512]{1,0:T(8,128)(2,1)S(1)}, u32[]{:S(2)}, u32[]{:S(2)}) collective-permute-start(bf16[1024,512]{1,0:T(8,128)(2,1)S(1)} %constant_dynamic-slice_fusion), channel_id=1, source_target_pairs={{0,20},{4,16},{8,28},{12,24},{16,4},{20,0},{24,12},{28,8},{1,21},{... | collective-permute-start | bytes 3145736 | tf_op jit(solution)/shard_map/ppermute | solution.py:287
  6.0 4.6 %pack.1 = (bf16[64,8,512]{2,1,0:T(8,128)(2,1)}, bf16[64,8,512]{2,1,0:T(8,128)(2,1)}) custom-call(s32[128]{0:T(128)} %dynamic_slice.6.owned, bf16[128,8,512]{2,1,0:T(8,128)(2,1)} %bitcast.54), custom_call_target="tpu_custom_call" | custom-call | flops 1048576 | bytes 2097152 | tf_op jit(solution)/shard_map/pack/pallas_call | solution.py:81
  10.6 17.4 %all-to-all-start = ((bf16[64,8,512]{2,1,0:T(8,128)(2,1)}), bf16[64,8,512]{2,1,0:T(8,128)(2,1)S(1)}, u32[]{:S(2)}, u32[]{:S(2)}) async-start(bf16[64,8,512]{2,1,0:T(8,128)(2,1)} %get-tuple-element.13), calls=%async_computation | async-start | bytes 1048576 | tf_op jit(solution)/shard_map/all_to_all | solution.py:293
  28.0 2.1 %collective-permute-start.6 = (bf16[512,512]{1,0:T(8,128)(2,1)}, bf16[512,512]{1,0:T(8,128)(2,1)S(1)}, u32[]{:S(2)}, u32[]{:S(2)}) collective-permute-start(bf16[512,512]{1,0:T(8,128)(2,1)} %bitcast.55), channel_id=1, source_target_pairs={{0,1},{1,2},{2,3},{3,0},{8,11},{9,8},{10,9},{11,10},{4,5},{5,6},{6... | collective-permute-start | bytes 1572872 | tf_op jit(solution)/shard_map/ppermute | solution.py:44
  30.2 2.3 %collective-permute-start.4 = (bf16[1024,512]{1,0:T(8,128)(2,1)S(1)}, bf16[1024,512]{1,0:T(8,128)(2,1)S(1)}, u32[]{:S(2)}, u32[]{:S(2)}) collective-permute-start(bf16[1024,512]{1,0:T(8,128)(2,1)S(1)} %collective-permute-done.3.w_mine), channel_id=1, source_target_pairs={{0,8},{8,0},{1,9},{9,1},{2,10},{10,2},{3,11},{11,3},{4,12},{12,4},... | collective-permute-start | bytes 3145736 | tf_op jit(solution)/shard_map/ppermute | solution.py:288
  32.5 3.4 %collective-permute-start.7 = (bf16[512,512]{1,0:T(8,128)(2,1)}, bf16[512,512]{1,0:T(8,128)(2,1)}, u32[]{:S(2)}, u32[]{:S(2)}) collective-permute-start(bf16[512,512]{1,0:T(8,128)(2,1)} %bitcast.56), channel_id=1, source_target_pairs={{0,3},{1,0},{2,1},{3,2},{8,9},{9,10},{10,11},{11,8},{4,7},{5,4},{6... | collective-permute-start | bytes 1572872 | tf_op jit(solution)/shard_map/ppermute | solution.py:45
  36.0 5.2 %collective-permute-done.6.p1 = bf16[512,512]{1,0:T(8,128)(2,1)S(1)} collective-permute-done((bf16[512,512]{1,0:T(8,128)(2,1)}, bf16[512,512]{1,0:T(8,128)(2,1)S(1)}, u32[]{:S(2)}, u32[]{:S(2)}) %collective-permute-start.6) | collective-permute-done | bytes 524320 | tf_op jit(solution)/shard_map/ppermute | solution.py:44
  41.2 1.9 %collective-permute-start.8 = (bf16[512,512]{1,0:T(8,128)(2,1)S(1)}, bf16[512,512]{1,0:T(8,128)(2,1)}, u32[]{:S(2)}, u32[]{:S(2)}) collective-permute-start(bf16[512,512]{1,0:T(8,128)(2,1)S(1)} %collective-permute-done.6.p1), channel_id=1, source_target_pairs={{0,1},{1,2},{2,3},{3,0},{8,11},{9,8},{10,9},{11,10},{4,5},{5,6},{6... | collective-permute-start | bytes 1572872 | tf_op jit(solution)/shard_map/ppermute | solution.py:46
  45.4 7.0 %collective-permute-done.8.p3 = bf16[512,512]{1,0:T(8,128)(2,1)} collective-permute-done((bf16[512,512]{1,0:T(8,128)(2,1)S(1)}, bf16[512,512]{1,0:T(8,128)(2,1)}, u32[]{:S(2)}, u32[]{:S(2)}) %collective-permute-start.8) | collective-permute-done | bytes 524320 | tf_op jit(solution)/shard_map/ppermute | solution.py:46
  53.4 9.7 %shard_map.47 = (f32[512,512]{1,0:T(8,128)}, f32[512,128]{1,0:T(8,128)}, bf16[65,8,512]{2,1,0:T(8,128)(2,1)}) custom-call(s32[9]{0:T(128)} %pad_add_fusion.2.where, bf16[512,512]{1,0:T(8,128)(2,1)} %bitcast.57, bf16[512,512]{1,0:T(8,128)(2,1)} %copy-done.6, bf16[512,512]{1,0:T(8,128)(2,1)} %collective-permute-done.7.p2, ...), custom_call_target="tpu_custom_call" | custom-call | flops 2147483648 | bytes 8388608 | tf_op jit(solution)/shard_map/pallas_call | solution.py:161
  63.1 2.3 %collective-permute-start.9 = (bf16[65,8,512]{2,1,0:T(8,128)(2,1)}, bf16[65,8,512]{2,1,0:T(8,128)(2,1)S(1)}, u32[]{:S(2)}, u32[]{:S(2)}) collective-permute-start(bf16[65,8,512]{2,1,0:T(8,128)(2,1)} %get-tuple-element.20), channel_id=1, source_target_pairs={{0,4},{4,0},{1,5},{5,1},{2,6},{6,2},{3,7},{7,3},{8,12},{12,8},{9,1... | collective-permute-start | bytes 1597448 | tf_op jit(solution)/shard_map/ppermute | solution.py:308
  65.3 2.7 %bitcast_reduce_fusion = f32[2,512]{1,0:T(2,128)S(1)} fusion(bf16[4096,512]{1,0:T(8,128)(2,1)} %w_own.3, f32[4096]{0:T(1024)S(1)} %copy-done.11), kind=kLoop, calls=%fused_computation.1 | loop fusion | flops 6290432 | bytes 4214784 | tf_op jit(solution)/shard_map/reduce_sum | solution.py:300
  68.8 11.1 %collective-permute-done.9.came = bf16[65,8,512]{2,1,0:T(8,128)(2,1)S(1)} collective-permute-done((bf16[65,8,512]{2,1,0:T(8,128)(2,1)}, bf16[65,8,512]{2,1,0:T(8,128)(2,1)S(1)}, u32[]{:S(2)}, u32[]{:S(2)}) %collective-permute-start.9) | collective-permute-done | bytes 532512 | tf_op jit(solution)/shard_map/ppermute | solution.py:308
  80.7 3.1 %sum_g.1 = bf16[64,8,512]{2,1,0:T(8,128)(2,1)} custom-call(f32[512,512]{1,0:T(8,128)} %get-tuple-element.18.kept, f32[512,128]{1,0:T(8,128)} %get-tuple-element.19.table, bf16[65,8,512]{2,1,0:T(8,128)(2,1)} %copy-done.5, f32[2,512]{1,0:T(2,128)} %broadcast_select_fusion.gain_sums), custom_call_target="tpu_custom_call" | custom-call | flops 4194304 | bytes 4194304 | tf_op jit(solution)/shard_map/sum_g/pallas_call | solution.py:223
  83.8 13.6 %all-to-all-start.1 = ((bf16[64,8,512]{2,1,0:T(8,128)(2,1)}), bf16[64,8,512]{2,1,0:T(8,128)(2,1)S(1)}, u32[]{:S(2)}, u32[]{:S(2)}) async-start(bf16[64,8,512]{2,1,0:T(8,128)(2,1)} %sum_g.1), calls=%async_computation.1 | async-start | bytes 1048576 | tf_op jit(solution)/shard_map/all_to_all | solution.py:310
  97.5 2.3 %collective-permute-start = (bf16[512,512]{1,0:T(8,128)(2,1)S(1)}, bf16[512,512]{1,0:T(8,128)(2,1)S(1)}, u32[]{:S(2)}, u32[]{:S(2)}) collective-permute-start(bf16[512,512]{1,0:T(8,128)(2,1)S(1)} %bitcast.51), channel_id=1, source_target_pairs={{0,1},{1,2},{2,3},{3,0},{8,11},{9,8},{10,9},{11,10},{4,5},{5,6},{6... | collective-permute-start | bytes 1572872 | tf_op jit(solution)/shard_map/ppermute | solution.py:44
  99.8 3.5 %collective-permute-start.1 = (bf16[512,512]{1,0:T(8,128)(2,1)S(1)}, bf16[512,512]{1,0:T(8,128)(2,1)S(1)}, u32[]{:S(2)}, u32[]{:S(2)}) collective-permute-start(bf16[512,512]{1,0:T(8,128)(2,1)S(1)} %bitcast.52), channel_id=1, source_target_pairs={{0,3},{1,0},{2,1},{3,2},{8,9},{9,10},{10,11},{11,8},{4,7},{5,4},{6... | collective-permute-start | bytes 1572872 | tf_op jit(solution)/shard_map/ppermute | solution.py:45
  103.3 9.8 %collective-permute-done.p1 = bf16[512,512]{1,0:T(8,128)(2,1)S(1)} collective-permute-done((bf16[512,512]{1,0:T(8,128)(2,1)S(1)}, bf16[512,512]{1,0:T(8,128)(2,1)S(1)}, u32[]{:S(2)}, u32[]{:S(2)}) %collective-permute-start) | collective-permute-done | bytes 524320 | tf_op jit(solution)/shard_map/ppermute | solution.py:44
  113.1 1.9 %collective-permute-start.2 = (bf16[512,512]{1,0:T(8,128)(2,1)S(1)}, bf16[512,512]{1,0:T(8,128)(2,1)S(1)}, u32[]{:S(2)}, u32[]{:S(2)}) collective-permute-start(bf16[512,512]{1,0:T(8,128)(2,1)S(1)} %collective-permute-done.p1), channel_id=1, source_target_pairs={{0,1},{1,2},{2,3},{3,0},{8,11},{9,8},{10,9},{11,10},{4,5},{5,6},{6... | collective-permute-start | bytes 1572872 | tf_op jit(solution)/shard_map/ppermute | solution.py:46
  115.0 9.1 %collective-permute-done.2.p3 = bf16[512,512]{1,0:T(8,128)(2,1)S(1)} collective-permute-done((bf16[512,512]{1,0:T(8,128)(2,1)S(1)}, bf16[512,512]{1,0:T(8,128)(2,1)S(1)}, u32[]{:S(2)}, u32[]{:S(2)}) %collective-permute-start.2) | collective-permute-done | bytes 524320 | tf_op jit(solution)/shard_map/ppermute | solution.py:46
  125.0 9.7 %shard_map.46 = (f32[512,512]{1,0:T(8,128)}, f32[512,128]{1,0:T(8,128)}, bf16[65,8,512]{2,1,0:T(8,128)(2,1)}) custom-call(s32[9]{0:T(128)} %pad_add_fusion.2.where, bf16[512,512]{1,0:T(8,128)(2,1)} %bitcast.53, bf16[512,512]{1,0:T(8,128)(2,1)} %copy-done.7, bf16[512,512]{1,0:T(8,128)(2,1)} %copy-done.8, bf16[512,512]{1,0:T(8,128)(2,1)} %copy-done.9, ...), custom_call_target="tpu_custom_call" | custom-call | flops 2147483648 | bytes 8388608 | tf_op jit(solution)/shard_map/pallas_call | solution.py:161
  134.6 3.8 %collective-permute-start.5 = (bf16[65,8,512]{2,1,0:T(8,128)(2,1)}, bf16[65,8,512]{2,1,0:T(8,128)(2,1)S(1)}, u32[]{:S(2)}, u32[]{:S(2)}) collective-permute-start(bf16[65,8,512]{2,1,0:T(8,128)(2,1)} %get-tuple-element.16), channel_id=1, source_target_pairs={{0,4},{4,0},{1,5},{5,1},{2,6},{6,2},{3,7},{7,3},{8,12},{12,8},{9,1... | collective-permute-start | bytes 1597448 | tf_op jit(solution)/shard_map/ppermute | solution.py:314
  139.3 11.6 %collective-permute-done.5.came = bf16[65,8,512]{2,1,0:T(8,128)(2,1)S(1)} collective-permute-done((bf16[65,8,512]{2,1,0:T(8,128)(2,1)}, bf16[65,8,512]{2,1,0:T(8,128)(2,1)S(1)}, u32[]{:S(2)}, u32[]{:S(2)}) %collective-permute-start.5) | collective-permute-done | bytes 532512 | tf_op jit(solution)/shard_map/ppermute | solution.py:314
  151.9 3.6 %place.1 = bf16[128,8,512]{2,1,0:T(8,128)(2,1)} custom-call(s32[128]{0:T(128)} %pad_add_fusion.slots, f32[512,512]{1,0:T(8,128)} %get-tuple-element.14.kept, f32[512,128]{1,0:T(8,128)} %get-tuple-element.15.table, bf16[65,8,512]{2,1,0:T(8,128)(2,1)} %copy-done.4, f32[2,512]{1,0:T(2,128)} %broadcast_select_fusion.gain_sums, bf16[64,8,512]{2,1,0:T(8,128)(2,1)} %copy-done.3), custom_call_target="tpu_custom_call" | custom-call | flops 4194304 | bytes 4194304 | tf_op jit(solution)/shard_map/place/pallas_call | solution.py:251
  (45 shorter events, 10.1 us)
Async XLA Ops:
  0.0 35.9 %copy-start.11 = (f32[4096]{0:T(1024)S(1)}, f32[4096]{0:T(1024)}, u32[]{:S(2)}) copy-start(f32[4096]{0:T(1024)} %param.5) | copy-start | bytes 49156
  1.3 28.9 %collective-permute-start.3 = (bf16[1024,512]{1,0:T(8,128)(2,1)S(1)}, bf16[1024,512]{1,0:T(8,128)(2,1)S(1)}, u32[]{:S(2)}, u32[]{:S(2)}) collective-permute-start(bf16[1024,512]{1,0:T(8,128)(2,1)S(1)} %constant_dynamic-slice_fusion), channel_id=1, source_target_pairs={{0,20},{4,16},{8,28},{12,24},{16,4},{20,0},{24,12},{28,8},{1,21},{... | collective-permute-start | bytes 3145736 | tf_op jit(solution)/shard_map/ppermute | solution.py:287
  10.6 73.3 %all-to-all-start = ((bf16[64,8,512]{2,1,0:T(8,128)(2,1)}), bf16[64,8,512]{2,1,0:T(8,128)(2,1)S(1)}, u32[]{:S(2)}, u32[]{:S(2)}) async-start(bf16[64,8,512]{2,1,0:T(8,128)(2,1)} %get-tuple-element.13), calls=%async_computation | async-start | bytes 1048576 | tf_op jit(solution)/shard_map/all_to_all | solution.py:293
  28.0 13.2 %collective-permute-start.6 = (bf16[512,512]{1,0:T(8,128)(2,1)}, bf16[512,512]{1,0:T(8,128)(2,1)S(1)}, u32[]{:S(2)}, u32[]{:S(2)}) collective-permute-start(bf16[512,512]{1,0:T(8,128)(2,1)} %bitcast.55), channel_id=1, source_target_pairs={{0,1},{1,2},{2,3},{3,0},{8,11},{9,8},{10,9},{11,10},{4,5},{5,6},{6... | collective-permute-start | bytes 1572872 | tf_op jit(solution)/shard_map/ppermute | solution.py:44
  30.2 22.2 %copy-start = (bf16[1024,512]{1,0:T(8,128)(2,1)}, bf16[1024,512]{1,0:T(8,128)(2,1)S(1)}, u32[]{:S(2)}) copy-start(bf16[1024,512]{1,0:T(8,128)(2,1)S(1)} %collective-permute-done.3.w_mine) | copy-start | bytes 3145732
  30.2 22.2 %collective-permute-start.4 = (bf16[1024,512]{1,0:T(8,128)(2,1)S(1)}, bf16[1024,512]{1,0:T(8,128)(2,1)S(1)}, u32[]{:S(2)}, u32[]{:S(2)}) collective-permute-start(bf16[1024,512]{1,0:T(8,128)(2,1)S(1)} %collective-permute-done.3.w_mine), channel_id=1, source_target_pairs={{0,8},{8,0},{1,9},{9,1},{2,10},{10,2},{3,11},{11,3},{4,12},{12,4},... | collective-permute-start | bytes 3145736 | tf_op jit(solution)/shard_map/ppermute | solution.py:288
  32.5 12.9 %collective-permute-start.7 = (bf16[512,512]{1,0:T(8,128)(2,1)}, bf16[512,512]{1,0:T(8,128)(2,1)}, u32[]{:S(2)}, u32[]{:S(2)}) collective-permute-start(bf16[512,512]{1,0:T(8,128)(2,1)} %bitcast.56), channel_id=1, source_target_pairs={{0,3},{1,0},{2,1},{3,2},{8,9},{9,10},{10,11},{11,8},{4,7},{5,4},{6... | collective-permute-start | bytes 1572872 | tf_op jit(solution)/shard_map/ppermute | solution.py:45
  41.2 11.2 %copy-start.6 = (bf16[512,512]{1,0:T(8,128)(2,1)}, bf16[512,512]{1,0:T(8,128)(2,1)S(1)}, u32[]{:S(2)}) copy-start(bf16[512,512]{1,0:T(8,128)(2,1)S(1)} %collective-permute-done.6.p1) | copy-start | bytes 1572868
  41.2 11.2 %collective-permute-start.8 = (bf16[512,512]{1,0:T(8,128)(2,1)S(1)}, bf16[512,512]{1,0:T(8,128)(2,1)}, u32[]{:S(2)}, u32[]{:S(2)}) collective-permute-start(bf16[512,512]{1,0:T(8,128)(2,1)S(1)} %collective-permute-done.6.p1), channel_id=1, source_target_pairs={{0,1},{1,2},{2,3},{3,0},{8,11},{9,8},{10,9},{11,10},{4,5},{5,6},{6... | collective-permute-start | bytes 1572872 | tf_op jit(solution)/shard_map/ppermute | solution.py:46
  52.4 1.0 copy-start.1
  63.1 16.8 %collective-permute-start.9 = (bf16[65,8,512]{2,1,0:T(8,128)(2,1)}, bf16[65,8,512]{2,1,0:T(8,128)(2,1)S(1)}, u32[]{:S(2)}, u32[]{:S(2)}) collective-permute-start(bf16[65,8,512]{2,1,0:T(8,128)(2,1)} %get-tuple-element.20), channel_id=1, source_target_pairs={{0,4},{4,0},{1,5},{5,1},{2,6},{6,2},{3,7},{7,3},{8,12},{12,8},{9,1... | collective-permute-start | bytes 1597448 | tf_op jit(solution)/shard_map/ppermute | solution.py:308
  79.9 0.8 copy-start.5
  83.8 40.3 %copy-start.2 = (bf16[64,8,512]{2,1,0:T(8,128)(2,1)}, bf16[64,8,512]{2,1,0:T(8,128)(2,1)S(1)}, u32[]{:S(2)}) copy-start(bf16[64,8,512]{2,1,0:T(8,128)(2,1)S(1)} %all-to-all-done) | copy-start | bytes 1572868
  83.8 67.1 %all-to-all-start.1 = ((bf16[64,8,512]{2,1,0:T(8,128)(2,1)}), bf16[64,8,512]{2,1,0:T(8,128)(2,1)S(1)}, u32[]{:S(2)}, u32[]{:S(2)}) async-start(bf16[64,8,512]{2,1,0:T(8,128)(2,1)} %sum_g.1), calls=%async_computation.1 | async-start | bytes 1048576 | tf_op jit(solution)/shard_map/all_to_all | solution.py:310
  97.5 40.9 %copy-start.10 = (s32[8192]{0:T(1024)S(1)}, s32[8192]{0:T(1024)}, u32[]{:S(2)}) copy-start(s32[8192]{0:T(1024)} %param.7) | copy-start | bytes 98308
  97.5 15.6 %collective-permute-start = (bf16[512,512]{1,0:T(8,128)(2,1)S(1)}, bf16[512,512]{1,0:T(8,128)(2,1)S(1)}, u32[]{:S(2)}, u32[]{:S(2)}) collective-permute-start(bf16[512,512]{1,0:T(8,128)(2,1)S(1)} %bitcast.51), channel_id=1, source_target_pairs={{0,1},{1,2},{2,3},{3,0},{8,11},{9,8},{10,9},{11,10},{4,5},{5,6},{6... | collective-permute-start | bytes 1572872 | tf_op jit(solution)/shard_map/ppermute | solution.py:44
  99.8 15.2 %collective-permute-start.1 = (bf16[512,512]{1,0:T(8,128)(2,1)S(1)}, bf16[512,512]{1,0:T(8,128)(2,1)S(1)}, u32[]{:S(2)}, u32[]{:S(2)}) collective-permute-start(bf16[512,512]{1,0:T(8,128)(2,1)S(1)} %bitcast.52), channel_id=1, source_target_pairs={{0,3},{1,0},{2,1},{3,2},{8,9},{9,10},{10,11},{11,8},{4,7},{5,4},{6... | collective-permute-start | bytes 1572872 | tf_op jit(solution)/shard_map/ppermute | solution.py:45
  113.1 11.1 %copy-start.7 = (bf16[512,512]{1,0:T(8,128)(2,1)}, bf16[512,512]{1,0:T(8,128)(2,1)S(1)}, u32[]{:S(2)}) copy-start(bf16[512,512]{1,0:T(8,128)(2,1)S(1)} %collective-permute-done.p1) | copy-start | bytes 1572868
  113.1 11.1 %collective-permute-start.2 = (bf16[512,512]{1,0:T(8,128)(2,1)S(1)}, bf16[512,512]{1,0:T(8,128)(2,1)S(1)}, u32[]{:S(2)}, u32[]{:S(2)}) collective-permute-start(bf16[512,512]{1,0:T(8,128)(2,1)S(1)} %collective-permute-done.p1), channel_id=1, source_target_pairs={{0,1},{1,2},{2,3},{3,0},{8,11},{9,8},{10,9},{11,10},{4,5},{5,6},{6... | collective-permute-start | bytes 1572872 | tf_op jit(solution)/shard_map/ppermute | solution.py:46
  115.0 9.1 %copy-start.8 = (bf16[512,512]{1,0:T(8,128)(2,1)}, bf16[512,512]{1,0:T(8,128)(2,1)S(1)}, u32[]{:S(2)}) copy-start(bf16[512,512]{1,0:T(8,128)(2,1)S(1)} %collective-permute-done.1.p2) | copy-start | bytes 1572868
  124.2 0.8 copy-start.9
  134.6 16.3 %collective-permute-start.5 = (bf16[65,8,512]{2,1,0:T(8,128)(2,1)}, bf16[65,8,512]{2,1,0:T(8,128)(2,1)S(1)}, u32[]{:S(2)}, u32[]{:S(2)}) collective-permute-start(bf16[65,8,512]{2,1,0:T(8,128)(2,1)} %get-tuple-element.16), channel_id=1, source_target_pairs={{0,4},{4,0},{1,5},{5,1},{2,6},{6,2},{3,7},{7,3},{8,12},{12,8},{9,1... | collective-permute-start | bytes 1597448 | tf_op jit(solution)/shard_map/ppermute | solution.py:314
  151.0 0.8 copy-start.4
  151.0 1.0 copy-start.3

commit v3 on v2

v3 whole, which is shorter than its diff:
```python
import functools

import jax
import jax.numpy as jnp
from jax import lax
from jax.experimental import pallas as pl
from jax.experimental.pallas import tpu as pltpu
from jax.sharding import Mesh
from jax.sharding import PartitionSpec as P

BLK = 8
EPS = 1e-05
TORUS = ("z", "xl", "c", "xh", "y")
SUBCUBE = ("xl", "c", "xh")
SPREAD = ("c", "z", "xl")
VMEM = pl.BlockSpec(memory_space=pltpu.VMEM)
SMEM = pl.BlockSpec(memory_space=pltpu.SMEM)
F32, BF16 = jnp.float32, jnp.bfloat16


def torus_mesh(mesh):
    groups, parts = mesh.devices.shape
    return Mesh(mesh.devices.reshape(groups // 4, 2, 2, 2, parts // 2), TORUS)


def crossing():
    return [
        ((xl * 2 + c) * 2 + xh, ((1 - xl) * 2 + c) * 2 + (1 - xh))
        for xl in range(2)
        for c in range(2)
        for xh in range(2)
    ]


def gather_y(piece):
    ring = lax.axis_size("y")

    def send(step):
        return lax.ppermute(piece, "y", [(y, (y + step) % ring) for y in range(ring)])

    far = send(2)
    near = send(1)
    other = send(-1)
    return [piece, far, near, other]


def pack_kernel(groups, table, rows, weights, first, second, leaving, count, staged, sems):
    blocks = rows.shape[0]
    shift = blocks.bit_length() - 1
    quarter = staged.shape[0]
    xh, core = lax.axis_index("xh"), lax.axis_index("c")
    group = lax.axis_index("z") * 4 + lax.axis_index("xl") * 2 + core
    base = group * blocks
    start = pl.multiple_of(((1 - xh) * 2 + core) * quarter, quarter)
    load = pltpu.make_async_copy(weights.at[pl.ds(start, quarter), :], staged, sems.at[0])
    store = pltpu.make_async_copy(staged, leaving, sems.at[1])
    load.start()

    def clear(i, carry):
        count[i] = 0
        return carry

    def put(b, carry):
        target = table[base + b] >> shift
        seen = count[target]
        count[target] = seen + 1
        spot = (target & 1) * (groups // 2) + (target >> 1)

        @pl.when(seen == 0)
        def _():
            first[spot] = rows[b]

        @pl.when(seen != 0)
        def _():
            second[spot] = rows[b]

        return carry

    lax.fori_loop(0, groups, clear, 0, unroll=8)
    lax.fori_loop(0, blocks // 2, put, 0, unroll=4)
    load.wait()
    store.start()
    lax.fori_loop(blocks // 2, blocks, put, 0, unroll=4)
    store.wait()


def grant(mib):
    return pltpu.CompilerParams(vmem_limit_bytes=mib << 20)


def cost():
    return pl.CostEstimate(flops=1 << 34, bytes_accessed=0, transcendentals=0)


ANY = pl.BlockSpec(memory_space=pl.ANY)


def pack(memory_rows, owner_table, key_weight, groups):
    rows, cols = memory_rows.shape
    width, outs = key_weight.shape
    blocks = rows // BLK
    out = jax.ShapeDtypeStruct((groups, BLK, cols), BF16)
    return pl.pallas_call(
        functools.partial(pack_kernel, groups),
        out_shape=(out, out, jax.ShapeDtypeStruct((width // 4, outs), BF16)),
        in_specs=[SMEM, VMEM, ANY],
        out_specs=(VMEM, VMEM, ANY),
        scratch_shapes=[
            pltpu.SMEM((groups,), jnp.int32),
            pltpu.VMEM((width // 4, outs), BF16),
            pltpu.SemaphoreType.DMA((2,)),
        ],
        cost_estimate=cost(),
        name="pack",
    )(owner_table, memory_rows.reshape(blocks, BLK, cols), key_weight)


def owners():
    y, ring = lax.axis_index("y"), lax.axis_size("y")
    return [y, lax.rem(y + 2, ring), lax.rem(y + ring - 1, ring), lax.rem(y + 1, ring)]


def gain_rows(gain):
    high = gain.astype(BF16).astype(F32)
    middle = (gain - high).astype(BF16).astype(F32)
    zeros = jnp.zeros((BLK - 3, gain.shape[1]), F32)
    return jnp.concatenate([high, middle, gain - high - middle, zeros], axis=0).astype(BF16)


def two_parts(value):
    high = value.astype(BF16).astype(F32)
    return high, value - high


def fold(value):
    lanes = [value[:, i : i + 128] for i in range(0, value.shape[1], 128)]
    return functools.reduce(jnp.add, lanes)


def sent_kernel(p0, p1, p2, p3, gains, w_mine, w_twin, table, sent, raw, scaled, held, sums, acc, sems):
    rows, width = p0.shape
    half = width * 4
    tile = 128
    tiles = rows // BLK
    xh, core = lax.axis_index("xh"), lax.axis_index("c")
    gain = [gains[xh * 4 + owner] for owner in owners()]
    piece_copies = [
        pltpu.make_async_copy(part, raw.at[j], sems.at[j]) for j, part in enumerate((p0, p1, p2, p3))
    ]
    deep = held.shape[0] // 2
    mine_copy = pltpu.make_async_copy(w_mine, held.at[0:deep], sems.at[4])
    twin_copy = pltpu.make_async_copy(w_twin, held.at[deep : 2 * deep], sems.at[5])
    for copy in piece_copies:
        copy.start()
    mine_copy.start()
    twin_copy.start()

    sent[tiles] = jnp.zeros(sent.shape[1:], BF16)
    for j in range(4):
        piece_copies[j].wait()
        for q in range(rows // tile):
            here = pl.ds(q * tile, tile)
            v = raw[j, here, :].astype(F32)
            total, square = fold(v), fold(v * v)
            if j == 0:
                sums[0, here], sums[1, here] = total, square
            else:
                sums[0, here] += total
                sums[1, here] += square
    for q in range(rows // tile):
        here = pl.ds(q * tile, tile)
        mean = jnp.sum(sums[0, here], axis=1, keepdims=True) / half
        square = jnp.sum(sums[1, here], axis=1, keepdims=True) / half
        center, rest = two_parts(mean)
        high, low = two_parts(square - mean * mean)
        for j in range(4):
            v = raw[j, here, :].astype(F32)
            scaled[j, here, :] = ((v - center) * gain[j]).astype(BF16)
        lane = lax.broadcasted_iota(jnp.int32, (tile, 128), 1)
        stats = jnp.where(lane == 0, center, 0.0)
        stats = jnp.where(lane == 1, rest, stats)
        stats = jnp.where(lane == 2, high, stats)
        stats = jnp.where(lane == 3, low, stats)
        table[here, :] = stats
        sent[tiles, :, q * 128 : (q + 1) * 128] = jnp.transpose(stats)[0:BLK, :].astype(BF16)

    mine_copy.wait()
    twin_copy.wait()
    gain_sum = jnp.zeros((BLK, acc.shape[1]), F32)
    for j, owner in enumerate(owners()):
        slot = ((owner >> 1) ^ core) * 2 + (owner & 1)
        block = held[pl.ds(pl.multiple_of(slot * width, width), width), :]
        gain_sum += jnp.dot(gain_rows(gain[j]), block, preferred_element_type=F32)
        part = jnp.dot(scaled[j], block, preferred_element_type=F32)
        if j == 0:
            acc[...] = part
        elif j < 3:
            acc[...] += part
        else:
            sent[0:tiles] = (acc[...] + part).reshape(tiles, BLK, part.shape[1]).astype(BF16)
    total = jnp.sum(gain_sum, axis=0, keepdims=True)
    high, rest = two_parts(total)
    middle, low = two_parts(rest)
    row = lax.broadcasted_iota(jnp.int32, (BLK, width), 0)
    extra = sent[tiles].astype(F32)
    for place, value in ((4, high), (5, middle), (6, low)):
        extra = jnp.where(row == place, value, extra)
    sent[tiles] = extra.astype(BF16)


def project_sent(pieces, gains, mine, twin):
    rows, width = pieces[0].shape
    tiles = rows // BLK
    deep, cols = mine.shape
    return pl.pallas_call(
        sent_kernel,
        out_shape=(
            jax.ShapeDtypeStruct((rows, 128), F32),
            jax.ShapeDtypeStruct((tiles + 1, BLK, cols), BF16),
        ),
        in_specs=[ANY] * 4 + [VMEM] + [ANY] * 2,
        out_specs=(VMEM, VMEM),
        scratch_shapes=[
            pltpu.VMEM((4, rows, width), BF16),
            pltpu.VMEM((4, rows, width), BF16),
            pltpu.VMEM((2 * deep, cols), BF16),
            pltpu.VMEM((2, rows, 128), F32),
            pltpu.VMEM((rows, cols), F32),
            pltpu.SemaphoreType.DMA((6,)),
        ],
        compiler_params=grant(12),
        cost_estimate=cost(),
    )(*pieces, gains, mine, twin)


def kept_kernel(half_id, p0, p1, p2, p3, table, gains, w_own, kept, gain_sums):
    width = p0.shape[1]
    center = table[:, 0:1]
    xh = lax.axis_index("xh")
    total = jnp.zeros((BLK, kept.shape[1]), F32)
    for j, (part, owner) in enumerate(zip((p0, p1, p2, p3), owners())):
        gain = gains[xh * 4 + owner]
        block = w_own[pl.ds(pl.multiple_of(owner * width, width), width), :]
        scaled = ((part[...].astype(F32) - center) * gain).astype(BF16)
        total += jnp.dot(gain_rows(gain), block, preferred_element_type=F32)
        product = jnp.dot(scaled, block, preferred_element_type=F32)
        if j == 0:
            kept[...] = product
        else:
            kept[...] += product
    gain_sums[...] = jnp.broadcast_to(jnp.sum(total, axis=0, keepdims=True), total.shape)


def project_kept(pieces, table, half_id, gains, key_weight):
    rows, width = pieces[0].shape
    half, cols = key_weight.shape[0] // 2, key_weight.shape[1]
    whole = pl.BlockSpec((rows, width), lambda i, s: (0, 0))
    return pl.pallas_call(
        kept_kernel,
        out_shape=(
            jax.ShapeDtypeStruct((rows, cols), F32),
            jax.ShapeDtypeStruct((BLK, cols), F32),
        ),
        grid_spec=pltpu.PrefetchScalarGridSpec(
            num_scalar_prefetch=1,
            grid=(1,),
            in_specs=[whole] * 4
            + [
                pl.BlockSpec((rows, 128), lambda i, s: (0, 0)),
                pl.BlockSpec(gains.shape, lambda i, s: (0, 0, 0)),
                pl.BlockSpec((half, cols), lambda i, s: (s[0], 0)),
            ],
            out_specs=(
                pl.BlockSpec((rows, cols), lambda i, s: (0, 0)),
                pl.BlockSpec((BLK, cols), lambda i, s: (0, 0)),
            ),
        ),
        compiler_params=grant(16),
        cost_estimate=cost(),
    )(half_id, *pieces, table, gains, key_weight)


def whole_keys(kept, table, came, gain_sums, q):
    tiles = came.shape[0] - 1
    cols = came.shape[2]
    here = pl.ds(q * 128, 128)
    per = 128 // BLK
    value_b = came[q * per : (q + 1) * per].astype(F32).reshape(128, cols)
    stats = came[tiles, :, q * 128 : (q + 1) * 128].astype(F32)
    stats = jnp.concatenate([stats, jnp.zeros((128 - BLK, 128), F32)], axis=0)
    stats_b = jnp.transpose(stats)
    stats_a = table[here, :]
    center_a, center_b = stats_a[:, 0:1], stats_b[:, 0:1]
    mean_a, mean_b = center_a + stats_a[:, 1:2], center_b + stats_b[:, 1:2]
    var_a, var_b = stats_a[:, 2:3] + stats_a[:, 3:4], stats_b[:, 2:3] + stats_b[:, 3:4]
    mean = 0.5 * (mean_a + mean_b)
    gap = 0.5 * (mean_a - mean_b)
    scale = lax.rsqrt(0.5 * (var_a + var_b) + gap * gap + EPS)
    sums_b = jnp.sum(came[tiles, 4:7, :].astype(F32), axis=0, keepdims=True)
    shift = (center_a - mean) * gain_sums[0:1, :] + (center_b - mean) * sums_b
    keys = (kept[here, :] + value_b + shift) * scale
    return keys.reshape(per, BLK, cols).astype(BF16)


def sum_kernel(kept, table, came, gain_sums, out):
    per = 128 // BLK
    for q in range(kept.shape[0] // 128):
        out[q * per : (q + 1) * per] = whole_keys(kept, table, came, gain_sums, q)


def sum_partials(kept, table, came, gain_sums):
    tiles, _, cols = came.shape
    return pl.pallas_call(
        sum_kernel,
        out_shape=jax.ShapeDtypeStruct((tiles - 1, BLK, cols), BF16),
        in_specs=[VMEM] * 4,
        out_specs=VMEM,
        compiler_params=grant(16),
        cost_estimate=cost(),
        name="sum_g",
    )(kept, table, came, gain_sums)


def place_kernel(slots, kept, table, came, gain_sums, others, out):
    groups = others.shape[0]
    per = 128 // BLK
    for q in range(kept.shape[0] // 128):
        keys = whole_keys(kept, table, came, gain_sums, q)
        for i in range(per):
            out[slots[q * per + i]] = keys[i]

    def put(i, carry):
        out[slots[groups + i]] = others[i]
        return carry

    lax.fori_loop(0, groups, put, 0, unroll=8)


def place(slots, kept, table, came, gain_sums, others):
    _, _, cols = came.shape
    blocks = slots.shape[0]
    return pl.pallas_call(
        place_kernel,
        out_shape=jax.ShapeDtypeStruct((blocks, BLK, cols), BF16),
        in_specs=[SMEM] + [VMEM] * 5,
        out_specs=VMEM,
        compiler_params=grant(16),
        cost_estimate=cost(),
        name="place",
    )(slots, kept, table, came, gain_sums, others)


def arrival_slots(owner_table, group, groups, blocks):
    table = owner_table.reshape(groups, blocks)
    ids = jnp.arange(blocks, dtype=jnp.int32)[None, :]
    here = table // blocks == group
    first = jnp.min(jnp.where(here, ids, blocks), axis=1, keepdims=True)
    slots = table % blocks
    slot_a = jnp.sum(jnp.where(ids == first, slots, 0), axis=1)
    slot_b = jnp.sum(jnp.where(here & (ids != first), slots, 0), axis=1)
    by_source = [
        slot.reshape(groups // 2, 2).T.reshape(groups) for slot in (slot_a, slot_b)
    ]
    return jnp.concatenate(by_source)


def steps(memory_rows, norm_gain, key_weight, owner_table):
    depth_z = lax.axis_size("z")
    groups = 4 * depth_z
    xh, core = lax.axis_index("xh"), lax.axis_index("c")
    group = lax.axis_index("z") * 4 + lax.axis_index("xl") * 2 + core
    rows, cols = memory_rows.shape
    blocks, half_rows = rows // BLK, rows // 2
    width, outs = key_weight.shape

    packed_p, packed_g, leaving = pack(memory_rows, owner_table, key_weight, groups)
    mine = lax.ppermute(leaving, SUBCUBE, crossing())
    twin = lax.ppermute(mine, "c", [(0, 1), (1, 0)])
    pieces_g = gather_y(packed_g.reshape(half_rows, cols))
    rows_p = lax.all_to_all(packed_p, SPREAD, 0, 0, tiled=True)

    gains = norm_gain.reshape(width // cols, 1, cols)
    half_id = xh.reshape(1).astype(jnp.int32)
    slots = arrival_slots(owner_table, group, groups, blocks)

    pair = [(0, 1), (1, 0)]
    table_g, sent_g = project_sent(pieces_g, gains, mine, twin)
    came_g = lax.ppermute(sent_g, "xh", pair)
    kept_g, gain_sums_g = project_kept(pieces_g, table_g, half_id, gains, key_weight)
    keys_g = sum_partials(kept_g, table_g, came_g, gain_sums_g)
    keys_g = lax.all_to_all(keys_g, SPREAD, 0, 0, tiled=True)

    pieces_p = gather_y(rows_p.reshape(half_rows, cols))
    table_p, sent_p = project_sent(pieces_p, gains, mine, twin)
    came_p = lax.ppermute(sent_p, "xh", pair)
    kept_p, gain_sums_p = project_kept(pieces_p, table_p, half_id, gains, key_weight)
    placed = place(slots, kept_p, table_p, came_p, gain_sums_p, keys_g)
    return placed.reshape(rows, outs)


def solution(mesh):
    groups, parts = ("z", "xl", "c"), ("xh", "y")
    torus = torus_mesh(mesh)
    return jax.shard_map(
        steps,
        mesh=torus,
        in_specs=(P(groups, parts), P(), P(None, parts), P()),
        out_specs=P(groups, parts),
        check_vma=False,
    )
```

time: 156 us -> 144 us (0.923)
  the two profiles are of different devices: /device:TPU:26 before, /device:TPU:63 now
where the time goes in v3:
time: 144 us; the launch traced here: 143 us
  starting transfers between devices  64.6 us (45%)
  waiting for transfers between devices  51.8 us (36%)
  Pallas kernels  22.7 us (16%)
  local copies, waits for them, and re-layouts  3.41 us (2%)
    ppermute x6, starting transfers between devices, send(): lax.ppermute(piece, 'y', [(y, (y + step) % ring) for y in range(ring)])  19.1 us
    all_to_all x1, starting transfers between devices, steps(): keys_g = lax.all_to_all(keys_g, SPREAD, 0, 0, tiled=True)  18.1 us
    all_to_all x1, starting transfers between devices, steps(): rows_p = lax.all_to_all(packed_p, SPREAD, 0, 0, tiled=True)  17.3 us
    ppermute x1, waiting for transfers between devices, steps(): came_p = lax.ppermute(sent_p, 'xh', pair)  14.7 us
    ppermute x1, waiting for transfers between devices, steps(): came_g = lax.ppermute(sent_g, 'xh', pair)  10.9 us
    all_to_all x1, waiting for transfers between devices, steps(): rows_p = lax.all_to_all(packed_p, SPREAD, 0, 0, tiled=True)  10.7 us
    ppermute x1, waiting for transfers between devices, steps(): mine = lax.ppermute(leaving, SUBCUBE, crossing())  7.89 us
    pallas_call x2, Pallas kernels, project_sent(): pl.pallas_call(sent_kernel, out_shape=(jax.ShapeDtypeStruct((rows, 128),...  7.84 us
  transfers between devices with their start and end apart: 12, of which 5 were waited for; matrix products, arithmetic and copies ran while one was open for 1% of the time, Pallas kernels for 11%

profile of v3, /device:TPU:63, one launch (start us, length us, event | category | flops | bytes accessed | tf_op | source)
XLA Modules:
  0.0 143.3 jit_solution(13532172830623358781)
XLA Ops:
  0.0 4.8 %pack.1 = (bf16[64,8,512]{2,1,0:T(8,128)(2,1)}, bf16[64,8,512]{2,1,0:T(8,128)(2,1)}, bf16[1024,512]{1,0:T(8,128)(2,1)}) custom-call(s32[8192]{0:T(1024)} %table.1, bf16[128,8,512]{2,1,0:T(8,128)(2,1)} %bitcast.58, bf16[4096,512]{1,0:T(8,128)(2,1)} %w_own.3), custom_call_target="tpu_custom_call" | custom-call | flops 17179869184 | tf_op jit(solution)/shard_map/pack/pallas_call | solution.py:103
  4.8 2.1 %collective-permute-start.3 = (bf16[1024,512]{1,0:T(8,128)(2,1)}, bf16[1024,512]{1,0:T(8,128)(2,1)S(1)}, u32[]{:S(2)}, u32[]{:S(2)}) collective-permute-start(bf16[1024,512]{1,0:T(8,128)(2,1)} %get-tuple-element.17), channel_id=1, source_target_pairs={{0,20},{4,16},{8,28},{12,24},{16,4},{20,0},{24,12},{28,8},{1,21},{... | collective-permute-start | bytes 3145736 | tf_op jit(solution)/shard_map/ppermute | solution.py:377
  6.9 17.3 %all-to-all-start = ((bf16[64,8,512]{2,1,0:T(8,128)(2,1)}), bf16[64,8,512]{2,1,0:T(8,128)(2,1)S(1)}, u32[]{:S(2)}, u32[]{:S(2)}) async-start(bf16[64,8,512]{2,1,0:T(8,128)(2,1)} %get-tuple-element.16), calls=%async_computation | async-start | bytes 1048576 | tf_op jit(solution)/shard_map/all_to_all | solution.py:380
  24.2 7.9 %collective-permute-done.3.w_mine = bf16[1024,512]{1,0:T(8,128)(2,1)S(1)} collective-permute-done((bf16[1024,512]{1,0:T(8,128)(2,1)}, bf16[1024,512]{1,0:T(8,128)(2,1)S(1)}, u32[]{:S(2)}, u32[]{:S(2)}) %collective-permute-start.3) | collective-permute-done | bytes 1048608 | tf_op jit(solution)/shard_map/ppermute | solution.py:377
  32.1 3.4 %collective-permute-start.4 = (bf16[1024,512]{1,0:T(8,128)(2,1)S(1)}, bf16[1024,512]{1,0:T(8,128)(2,1)S(1)}, u32[]{:S(2)}, u32[]{:S(2)}) collective-permute-start(bf16[1024,512]{1,0:T(8,128)(2,1)S(1)} %collective-permute-done.3.w_mine), channel_id=1, source_target_pairs={{0,8},{8,0},{1,9},{9,1},{2,10},{10,2},{3,11},{11,3},{4,12},{12,4},... | collective-permute-start | bytes 3145736 | tf_op jit(solution)/shard_map/ppermute | solution.py:378
  35.6 2.9 %collective-permute-start.6 = (bf16[512,512]{1,0:T(8,128)(2,1)}, bf16[512,512]{1,0:T(8,128)(2,1)S(1)}, u32[]{:S(2)}, u32[]{:S(2)}) collective-permute-start(bf16[512,512]{1,0:T(8,128)(2,1)} %bitcast.47), channel_id=1, source_target_pairs={{0,2},{1,3},{2,0},{3,1},{4,6},{5,7},{6,4},{7,5},{8,10},{9,11},{10,... | collective-permute-start | bytes 1572872 | tf_op jit(solution)/shard_map/ppermute | solution.py:39
  38.4 3.8 %collective-permute-start.7 = (bf16[512,512]{1,0:T(8,128)(2,1)}, bf16[512,512]{1,0:T(8,128)(2,1)}, u32[]{:S(2)}, u32[]{:S(2)}) collective-permute-start(bf16[512,512]{1,0:T(8,128)(2,1)} %bitcast.48), channel_id=1, source_target_pairs={{0,1},{1,2},{2,3},{3,0},{4,5},{5,6},{6,7},{7,4},{8,9},{9,10},{10,1... | collective-permute-start | bytes 1572872 | tf_op jit(solution)/shard_map/ppermute | solution.py:39
  42.2 1.9 %collective-permute-start.8 = (bf16[512,512]{1,0:T(8,128)(2,1)}, bf16[512,512]{1,0:T(8,128)(2,1)}, u32[]{:S(2)}, u32[]{:S(2)}) collective-permute-start(bf16[512,512]{1,0:T(8,128)(2,1)} %bitcast.49), channel_id=1, source_target_pairs={{0,3},{1,0},{2,1},{3,2},{4,7},{5,4},{6,5},{7,6},{8,11},{9,8},{10,9... | collective-permute-start | bytes 1572872 | tf_op jit(solution)/shard_map/ppermute | solution.py:39
  45.1 10.7 %all-to-all-done = bf16[64,8,512]{2,1,0:T(8,128)(2,1)S(1)} async-done(((bf16[64,8,512]{2,1,0:T(8,128)(2,1)}), bf16[64,8,512]{2,1,0:T(8,128)(2,1)S(1)}, u32[]{:S(2)}, u32[]{:S(2)}) %all-to-all-start) | async-done | bytes 524320 | tf_op jit(solution)/shard_map/all_to_all | solution.py:380
  55.8 2.9 %collective-permute-start = (bf16[512,512]{1,0:T(8,128)(2,1)S(1)}, bf16[512,512]{1,0:T(8,128)(2,1)}, u32[]{:S(2)}, u32[]{:S(2)}) collective-permute-start(bf16[512,512]{1,0:T(8,128)(2,1)S(1)} %bitcast.42), channel_id=1, source_target_pairs={{0,2},{1,3},{2,0},{3,1},{4,6},{5,7},{6,4},{7,5},{8,10},{9,11},{10,... | collective-permute-start | bytes 1572872 | tf_op jit(solution)/shard_map/ppermute | solution.py:39
  59.5 3.8 %collective-permute-start.1 = (bf16[512,512]{1,0:T(8,128)(2,1)S(1)}, bf16[512,512]{1,0:T(8,128)(2,1)}, u32[]{:S(2)}, u32[]{:S(2)}) collective-permute-start(bf16[512,512]{1,0:T(8,128)(2,1)S(1)} %bitcast.43), channel_id=1, source_target_pairs={{0,1},{1,2},{2,3},{3,0},{4,5},{5,6},{6,7},{7,4},{8,9},{9,10},{10,1... | collective-permute-start | bytes 1572872 | tf_op jit(solution)/shard_map/ppermute | solution.py:39
  63.3 3.9 %collective-permute-start.2 = (bf16[512,512]{1,0:T(8,128)(2,1)S(1)}, bf16[512,512]{1,0:T(8,128)(2,1)}, u32[]{:S(2)}, u32[]{:S(2)}) collective-permute-start(bf16[512,512]{1,0:T(8,128)(2,1)S(1)} %bitcast.44), channel_id=1, source_target_pairs={{0,3},{1,0},{2,1},{3,2},{4,7},{5,4},{6,5},{7,6},{8,11},{9,8},{10,9... | collective-permute-start | bytes 1572872 | tf_op jit(solution)/shard_map/ppermute | solution.py:39
  69.3 3.8 %shard_map.48 = (f32[512,128]{1,0:T(8,128)S(1)}, bf16[65,8,512]{2,1,0:T(8,128)(2,1)S(1)}) custom-call(bf16[512,512]{1,0:T(8,128)(2,1)S(1)} %bitcast.50, bf16[512,512]{1,0:T(8,128)(2,1)S(1)} %copy-done.5, bf16[512,512]{1,0:T(8,128)(2,1)} %collective-permute-done.7.p2, bf16[512,512]{1,0:T(8,128)(2,1)} %collective-permute-done.8.p3, f32[8,1,512]{2,1,0:T(1,128)S(1)} %bitcast.52, ...), custom_call_target="tpu_custom_call" | custom-call | flops 17179869184 | tf_op jit(solution)/shard_map/pallas_call | solution.py:215
  73.1 2.4 %collective-permute-start.9 = (bf16[65,8,512]{2,1,0:T(8,128)(2,1)S(1)}, bf16[65,8,512]{2,1,0:T(8,128)(2,1)S(1)}, u32[]{:S(2)}, u32[]{:S(2)}) collective-permute-start(bf16[65,8,512]{2,1,0:T(8,128)(2,1)S(1)} %get-tuple-element.25), channel_id=1, source_target_pairs={{0,4},{4,0},{1,5},{5,1},{2,6},{6,2},{3,7},{7,3},{8,12},{12,8},{9,1... | collective-permute-start | bytes 1597448 | tf_op jit(solution)/shard_map/ppermute | solution.py:388
  75.6 2.9 %shard_map.49 = (f32[512,512]{1,0:T(8,128)S(1)}, f32[8,512]{1,0:T(8,128)S(1)}) custom-call(s32[1]{0:T(128)} %bitcast.3.half_id, bf16[512,512]{1,0:T(8,128)(2,1)S(1)} %bitcast.51, bf16[512,512]{1,0:T(8,128)(2,1)S(1)} %copy-done.6, bf16[512,512]{1,0:T(8,128)(2,1)} %collective-permute-done.7.p2, bf16[512,512]{1,0:T(8,128)(2,1)} %collective-permute-done.8.p3, ...), custom_call_target="tpu_custom_call" | custom-call | flops 17179869184 | tf_op jit(solution)/shard_map/pallas_call | solution.py:258
  78.5 10.9 %collective-permute-done.9.came = bf16[65,8,512]{2,1,0:T(8,128)(2,1)S(1)} collective-permute-done((bf16[65,8,512]{2,1,0:T(8,128)(2,1)S(1)}, bf16[65,8,512]{2,1,0:T(8,128)(2,1)S(1)}, u32[]{:S(2)}, u32[]{:S(2)}) %collective-permute-start.9) | collective-permute-done | bytes 532512 | tf_op jit(solution)/shard_map/ppermute | solution.py:388
  89.3 1.7 %sum_g.1 = bf16[64,8,512]{2,1,0:T(8,128)(2,1)} custom-call(f32[512,512]{1,0:T(8,128)S(1)} %get-tuple-element.24.kept, f32[512,128]{1,0:T(8,128)S(1)} %get-tuple-element.23.table, bf16[65,8,512]{2,1,0:T(8,128)(2,1)S(1)} %collective-permute-done.9.came, f32[8,512]{1,0:T(8,128)S(1)} %get-tuple-element.26.gain_sums), custom_call_target="tpu_custom_call" | custom-call | flops 17179869184 | tf_op jit(solution)/shard_map/sum_g/pallas_call | solution.py:313
  91.0 18.1 %all-to-all-start.1 = ((bf16[64,8,512]{2,1,0:T(8,128)(2,1)}), bf16[64,8,512]{2,1,0:T(8,128)(2,1)S(1)}, u32[]{:S(2)}, u32[]{:S(2)}) async-start(bf16[64,8,512]{2,1,0:T(8,128)(2,1)} %sum_g.1), calls=%async_computation.1 | async-start | bytes 1048576 | tf_op jit(solution)/shard_map/all_to_all | solution.py:391
  109.2 4.0 %shard_map.46 = (f32[512,128]{1,0:T(8,128)S(1)}, bf16[65,8,512]{2,1,0:T(8,128)(2,1)S(1)}) custom-call(bf16[512,512]{1,0:T(8,128)(2,1)S(1)} %bitcast.45, bf16[512,512]{1,0:T(8,128)(2,1)} %collective-permute-done.p1, bf16[512,512]{1,0:T(8,128)(2,1)} %collective-permute-done.1.p2, bf16[512,512]{1,0:T(8,128)(2,1)} %collective-permute-done.2.p3, ...), custom_call_target="tpu_custom_call" | custom-call | flops 17179869184 | tf_op jit(solution)/shard_map/pallas_call | solution.py:215
  113.2 2.1 %collective-permute-start.5 = (bf16[65,8,512]{2,1,0:T(8,128)(2,1)S(1)}, bf16[65,8,512]{2,1,0:T(8,128)(2,1)S(1)}, u32[]{:S(2)}, u32[]{:S(2)}) collective-permute-start(bf16[65,8,512]{2,1,0:T(8,128)(2,1)S(1)} %get-tuple-element.20), channel_id=1, source_target_pairs={{0,4},{4,0},{1,5},{5,1},{2,6},{6,2},{3,7},{7,3},{8,12},{12,8},{9,1... | collective-permute-start | bytes 1597448 | tf_op jit(solution)/shard_map/ppermute | solution.py:395
  115.3 3.0 %shard_map.47 = (f32[512,512]{1,0:T(8,128)S(1)}, f32[8,512]{1,0:T(8,128)S(1)}) custom-call(s32[1]{0:T(128)} %bitcast.3.half_id, bf16[512,512]{1,0:T(8,128)(2,1)S(1)} %bitcast.46, bf16[512,512]{1,0:T(8,128)(2,1)} %collective-permute-done.p1, bf16[512,512]{1,0:T(8,128)(2,1)} %collective-permute-done.1.p2, bf16[512,512]{1,0:T(8,128)(2,1)} %collective-permute-done.2.p3, ...), custom_call_target="tpu_custom_call" | custom-call | flops 17179869184 | tf_op jit(solution)/shard_map/pallas_call | solution.py:258
  118.3 14.7 %collective-permute-done.5.came = bf16[65,8,512]{2,1,0:T(8,128)(2,1)S(1)} collective-permute-done((bf16[65,8,512]{2,1,0:T(8,128)(2,1)S(1)}, bf16[65,8,512]{2,1,0:T(8,128)(2,1)S(1)}, u32[]{:S(2)}, u32[]{:S(2)}) %collective-permute-start.5) | collective-permute-done | bytes 532512 | tf_op jit(solution)/shard_map/ppermute | solution.py:395
  133.1 7.6 %all-to-all-done.1.others = bf16[64,8,512]{2,1,0:T(8,128)(2,1)S(1)} async-done(((bf16[64,8,512]{2,1,0:T(8,128)(2,1)}), bf16[64,8,512]{2,1,0:T(8,128)(2,1)S(1)}, u32[]{:S(2)}, u32[]{:S(2)}) %all-to-all-start.1) | async-done | bytes 524320 | tf_op jit(solution)/shard_map/all_to_all | solution.py:391
  140.7 2.6 %place.1 = bf16[128,8,512]{2,1,0:T(8,128)(2,1)} custom-call(s32[128]{0:T(128)S(1)} %pad_add_fusion.slots, f32[512,512]{1,0:T(8,128)S(1)} %get-tuple-element.19.kept, f32[512,128]{1,0:T(8,128)S(1)} %get-tuple-element.18.table, bf16[65,8,512]{2,1,0:T(8,128)(2,1)S(1)} %collective-permute-done.5.came, f32[8,512]{1,0:T(8,128)S(1)} %get-tuple-element.21.gain_sums, ...), custom_call_target="tpu_custom_call" | custom-call | flops 17179869184 | tf_op jit(solution)/shard_map/place/pallas_call | solution.py:342
  (34 shorter events, 3.8 us)
Async XLA Ops:
  0.0 44.2 %copy-start.8 = (s32[8192]{0:T(1024)S(1)}, s32[8192]{0:T(1024)}, u32[]{:S(2)}) copy-start(s32[8192]{0:T(1024)} %table.1) | copy-start | bytes 98308
  0.0 67.2 %copy-start.7 = (f32[4096]{0:T(1024)S(1)}, f32[4096]{0:T(1024)}, u32[]{:S(2)}) copy-start(f32[4096]{0:T(1024)} %param.5) | copy-start | bytes 49156
  4.8 27.4 %collective-permute-start.3 = (bf16[1024,512]{1,0:T(8,128)(2,1)}, bf16[1024,512]{1,0:T(8,128)(2,1)S(1)}, u32[]{:S(2)}, u32[]{:S(2)}) collective-permute-start(bf16[1024,512]{1,0:T(8,128)(2,1)} %get-tuple-element.17), channel_id=1, source_target_pairs={{0,20},{4,16},{8,28},{12,24},{16,4},{20,0},{24,12},{28,8},{1,21},{... | collective-permute-start | bytes 3145736 | tf_op jit(solution)/shard_map/ppermute | solution.py:377
  6.9 48.9 %all-to-all-start = ((bf16[64,8,512]{2,1,0:T(8,128)(2,1)}), bf16[64,8,512]{2,1,0:T(8,128)(2,1)S(1)}, u32[]{:S(2)}, u32[]{:S(2)}) async-start(bf16[64,8,512]{2,1,0:T(8,128)(2,1)} %get-tuple-element.16), calls=%async_computation | async-start | bytes 1048576 | tf_op jit(solution)/shard_map/all_to_all | solution.py:380
  32.1 35.1 %collective-permute-start.4 = (bf16[1024,512]{1,0:T(8,128)(2,1)S(1)}, bf16[1024,512]{1,0:T(8,128)(2,1)S(1)}, u32[]{:S(2)}, u32[]{:S(2)}) collective-permute-start(bf16[1024,512]{1,0:T(8,128)(2,1)S(1)} %collective-permute-done.3.w_mine), channel_id=1, source_target_pairs={{0,8},{8,0},{1,9},{9,1},{2,10},{10,2},{3,11},{11,3},{4,12},{12,4},... | collective-permute-start | bytes 3145736 | tf_op jit(solution)/shard_map/ppermute | solution.py:378
  35.6 23.1 %collective-permute-start.6 = (bf16[512,512]{1,0:T(8,128)(2,1)}, bf16[512,512]{1,0:T(8,128)(2,1)S(1)}, u32[]{:S(2)}, u32[]{:S(2)}) collective-permute-start(bf16[512,512]{1,0:T(8,128)(2,1)} %bitcast.47), channel_id=1, source_target_pairs={{0,2},{1,3},{2,0},{3,1},{4,6},{5,7},{6,4},{7,5},{8,10},{9,11},{10,... | collective-permute-start | bytes 1572872 | tf_op jit(solution)/shard_map/ppermute | solution.py:39
  38.4 24.8 %collective-permute-start.7 = (bf16[512,512]{1,0:T(8,128)(2,1)}, bf16[512,512]{1,0:T(8,128)(2,1)}, u32[]{:S(2)}, u32[]{:S(2)}) collective-permute-start(bf16[512,512]{1,0:T(8,128)(2,1)} %bitcast.48), channel_id=1, source_target_pairs={{0,1},{1,2},{2,3},{3,0},{4,5},{5,6},{6,7},{7,4},{8,9},{9,10},{10,1... | collective-permute-start | bytes 1572872 | tf_op jit(solution)/shard_map/ppermute | solution.py:39
  42.2 24.9 %collective-permute-start.8 = (bf16[512,512]{1,0:T(8,128)(2,1)}, bf16[512,512]{1,0:T(8,128)(2,1)}, u32[]{:S(2)}, u32[]{:S(2)}) collective-permute-start(bf16[512,512]{1,0:T(8,128)(2,1)} %bitcast.49), channel_id=1, source_target_pairs={{0,3},{1,0},{2,1},{3,2},{4,7},{5,4},{6,5},{7,6},{8,11},{9,8},{10,9... | collective-permute-start | bytes 1572872 | tf_op jit(solution)/shard_map/ppermute | solution.py:39
  55.8 53.4 %collective-permute-start = (bf16[512,512]{1,0:T(8,128)(2,1)S(1)}, bf16[512,512]{1,0:T(8,128)(2,1)}, u32[]{:S(2)}, u32[]{:S(2)}) collective-permute-start(bf16[512,512]{1,0:T(8,128)(2,1)S(1)} %bitcast.42), channel_id=1, source_target_pairs={{0,2},{1,3},{2,0},{3,1},{4,6},{5,7},{6,4},{7,5},{8,10},{9,11},{10,... | collective-permute-start | bytes 1572872 | tf_op jit(solution)/shard_map/ppermute | solution.py:39
  58.7 0.8 copy-start.4
  59.5 49.7 %collective-permute-start.1 = (bf16[512,512]{1,0:T(8,128)(2,1)S(1)}, bf16[512,512]{1,0:T(8,128)(2,1)}, u32[]{:S(2)}, u32[]{:S(2)}) collective-permute-start(bf16[512,512]{1,0:T(8,128)(2,1)S(1)} %bitcast.43), channel_id=1, source_target_pairs={{0,1},{1,2},{2,3},{3,0},{4,5},{5,6},{6,7},{7,4},{8,9},{9,10},{10,1... | collective-permute-start | bytes 1572872 | tf_op jit(solution)/shard_map/ppermute | solution.py:39
  63.3 45.9 %collective-permute-start.2 = (bf16[512,512]{1,0:T(8,128)(2,1)S(1)}, bf16[512,512]{1,0:T(8,128)(2,1)}, u32[]{:S(2)}, u32[]{:S(2)}) collective-permute-start(bf16[512,512]{1,0:T(8,128)(2,1)S(1)} %bitcast.44), channel_id=1, source_target_pairs={{0,3},{1,0},{2,1},{3,2},{4,7},{5,4},{6,5},{7,6},{8,11},{9,8},{10,9... | collective-permute-start | bytes 1572872 | tf_op jit(solution)/shard_map/ppermute | solution.py:39
  67.2 1.0 copy-start.2
  68.2 1.0 copy-start.5
  69.3 6.3 %copy-start = (bf16[4096,512]{1,0:T(8,128)(2,1)S(1)}, bf16[4096,512]{1,0:T(8,128)(2,1)}, u32[]{:S(2)}) copy-start(bf16[4096,512]{1,0:T(8,128)(2,1)} %w_own.3) | copy-start | bytes 12582916
  69.3 6.3 %copy-start.3 = (bf16[64,8,512]{2,1,0:T(8,128)(2,1)S(1)}, bf16[64,8,512]{2,1,0:T(8,128)(2,1)}, u32[]{:S(2)}) copy-start(bf16[64,8,512]{2,1,0:T(8,128)(2,1)} %get-tuple-element.22) | copy-start | bytes 1572868
  69.3 6.3 %copy-start.6 = (bf16[512,512]{1,0:T(8,128)(2,1)S(1)}, bf16[512,512]{1,0:T(8,128)(2,1)}, u32[]{:S(2)}) copy-start(bf16[512,512]{1,0:T(8,128)(2,1)} %copy-done.4) | copy-start | bytes 1572868
  73.1 16.2 %collective-permute-start.9 = (bf16[65,8,512]{2,1,0:T(8,128)(2,1)S(1)}, bf16[65,8,512]{2,1,0:T(8,128)(2,1)S(1)}, u32[]{:S(2)}, u32[]{:S(2)}) collective-permute-start(bf16[65,8,512]{2,1,0:T(8,128)(2,1)S(1)} %get-tuple-element.25), channel_id=1, source_target_pairs={{0,4},{4,0},{1,5},{5,1},{2,6},{6,2},{3,7},{7,3},{8,12},{12,8},{9,1... | collective-permute-start | bytes 1597448 | tf_op jit(solution)/shard_map/ppermute | solution.py:388
  91.0 49.7 %all-to-all-start.1 = ((bf16[64,8,512]{2,1,0:T(8,128)(2,1)}), bf16[64,8,512]{2,1,0:T(8,128)(2,1)S(1)}, u32[]{:S(2)}, u32[]{:S(2)}) async-start(bf16[64,8,512]{2,1,0:T(8,128)(2,1)} %sum_g.1), calls=%async_computation.1 | async-start | bytes 1048576 | tf_op jit(solution)/shard_map/all_to_all | solution.py:391
  109.1 6.2 %copy-start.1 = (bf16[4096,512]{1,0:T(8,128)(2,1)S(1)}, bf16[4096,512]{1,0:T(8,128)(2,1)}, u32[]{:S(2)}) copy-start(bf16[4096,512]{1,0:T(8,128)(2,1)} %w_own.3) | copy-start | bytes 12582916
  113.2 19.9 %collective-permute-start.5 = (bf16[65,8,512]{2,1,0:T(8,128)(2,1)S(1)}, bf16[65,8,512]{2,1,0:T(8,128)(2,1)S(1)}, u32[]{:S(2)}, u32[]{:S(2)}) collective-permute-start(bf16[65,8,512]{2,1,0:T(8,128)(2,1)S(1)} %get-tuple-element.20), channel_id=1, source_target_pairs={{0,4},{4,0},{1,5},{5,1},{2,6},{6,2},{3,7},{7,3},{8,12},{12,8},{9,1... | collective-permute-start | bytes 1597448 | tf_op jit(solution)/shard_map/ppermute | solution.py:395

commit v4 on v3

--- a/solution.py
+++ b/solution.py
@@ -10,9 +10,9 @@
 
 BLK = 8
 EPS = 1e-05
-TORUS = ("z", "xl", "c", "xh", "y")
+TORUS = ("za", "zb", "xl", "c", "xh", "y")
 SUBCUBE = ("xl", "c", "xh")
-SPREAD = ("c", "z", "xl")
+SPREAD = ("c", "zb", "za", "xl")
 VMEM = pl.BlockSpec(memory_space=pltpu.VMEM)
 SMEM = pl.BlockSpec(memory_space=pltpu.SMEM)
 F32, BF16 = jnp.float32, jnp.bfloat16
@@ -20,7 +20,7 @@
 
 def torus_mesh(mesh):
     groups, parts = mesh.devices.shape
-    return Mesh(mesh.devices.reshape(groups // 4, 2, 2, 2, parts // 2), TORUS)
+    return Mesh(mesh.devices.reshape(groups // 16, 4, 2, 2, 2, parts // 2), TORUS)
 
 
 def crossing():
@@ -44,16 +44,30 @@
     return [piece, far, near, other]
 
 
-def pack_kernel(groups, table, rows, weights, first, second, leaving, count, staged, sems):
+def group_index():
+    z = lax.axis_index("za") * 4 + lax.axis_index("zb")
+    return z * 4 + lax.axis_index("xl") * 2 + lax.axis_index("c")
+
+
+def order_of(group, groups):
+    near = ((group >> 2) & 3) * (groups // 8) + (group >> 4) * 2
+    return (group & 1) * (groups // 2) + near + ((group >> 1) & 1)
+
+
+def pack_kernel(groups, table, rows_in, weights, first, second, leaving, count, rows, staged, sems):
     blocks = rows.shape[0]
     shift = blocks.bit_length() - 1
     quarter = staged.shape[0]
+    part = blocks // 4
     xh, core = lax.axis_index("xh"), lax.axis_index("c")
-    group = lax.axis_index("z") * 4 + lax.axis_index("xl") * 2 + core
-    base = group * blocks
+    base = group_index() * blocks
     start = pl.multiple_of(((1 - xh) * 2 + core) * quarter, quarter)
-    load = pltpu.make_async_copy(weights.at[pl.ds(start, quarter), :], staged, sems.at[0])
-    store = pltpu.make_async_copy(staged, leaving, sems.at[1])
+    pieces = [slice(i * part, (i + 1) * part) for i in range(4)]
+    loads = [pltpu.make_async_copy(rows_in.at[at], rows.at[at], sems.at[i]) for i, at in enumerate(pieces)]
+    load = pltpu.make_async_copy(weights.at[pl.ds(start, quarter), :], staged, sems.at[4])
+    store = pltpu.make_async_copy(staged, leaving, sems.at[5])
+    for copy in loads:
+        copy.start()
     load.start()
 
     def clear(i, carry):
@@ -64,23 +78,27 @@
         target = table[base + b] >> shift
         seen = count[target]
         count[target] = seen + 1
-        spot = (target & 1) * (groups // 2) + (target >> 1)
+        spot = order_of(target, groups)
 
         @pl.when(seen == 0)
         def _():
-            first[spot] = rows[b]
+            pltpu.make_async_copy(rows.at[b], first.at[spot], sems.at[6]).start()
 
         @pl.when(seen != 0)
         def _():
-            second[spot] = rows[b]
+            pltpu.make_async_copy(rows.at[b], second.at[spot], sems.at[7]).start()
 
         return carry
 
     lax.fori_loop(0, groups, clear, 0, unroll=8)
-    lax.fori_loop(0, blocks // 2, put, 0, unroll=4)
-    load.wait()
-    store.start()
-    lax.fori_loop(blocks // 2, blocks, put, 0, unroll=4)
+    for i in range(4):
+        loads[i].wait()
+        lax.fori_loop(i * part, (i + 1) * part, put, 0, unroll=4)
+        if i == 2:
+            load.wait()
+            store.start()
+    pltpu.make_async_copy(rows.at[0:groups], first, sems.at[6]).wait()
+    pltpu.make_async_copy(rows.at[0:groups], second, sems.at[7]).wait()
     store.wait()
 
 
@@ -103,12 +121,13 @@
     return pl.pallas_call(
         functools.partial(pack_kernel, groups),
         out_shape=(out, out, jax.ShapeDtypeStruct((width // 4, outs), BF16)),
-        in_specs=[SMEM, VMEM, ANY],
-        out_specs=(VMEM, VMEM, ANY),
+        in_specs=[SMEM, ANY, ANY],
+        out_specs=(ANY, ANY, ANY),
         scratch_shapes=[
             pltpu.SMEM((groups,), jnp.int32),
+            pltpu.VMEM((blocks, BLK, cols), BF16),
             pltpu.VMEM((width // 4, outs), BF16),
-            pltpu.SemaphoreType.DMA((2,)),
+            pltpu.SemaphoreType.DMA((8,)),
         ],
         cost_estimate=cost(),
         name="pack",
@@ -359,16 +378,14 @@
     slot_a = jnp.sum(jnp.where(ids == first, slots, 0), axis=1)
     slot_b = jnp.sum(jnp.where(here & (ids != first), slots, 0), axis=1)
     by_source = [
-        slot.reshape(groups // 2, 2).T.reshape(groups) for slot in (slot_a, slot_b)
+        slot.reshape(groups // 16, 4, 2, 2).transpose(3, 1, 0, 2).reshape(groups) for slot in (slot_a, slot_b)
     ]
     return jnp.concatenate(by_source)
 
 
 def steps(memory_rows, norm_gain, key_weight, owner_table):
-    depth_z = lax.axis_size("z")
-    groups = 4 * depth_z
-    xh, core = lax.axis_index("xh"), lax.axis_index("c")
-    group = lax.axis_index("z") * 4 + lax.axis_index("xl") * 2 + core
+    groups = owner_table.shape[0] // (memory_rows.shape[0] // BLK)
+    xh, group = lax.axis_index("xh"), group_index()
     rows, cols = memory_rows.shape
     blocks, half_rows = rows // BLK, rows // 2
     width, outs = key_weight.shape
@@ -399,7 +416,7 @@
 
 
 def solution(mesh):
-    groups, parts = ("z", "xl", "c"), ("xh", "y")
+    groups, parts = ("za", "zb", "xl", "c"), ("xh", "y")
     torus = torus_mesh(mesh)
     return jax.shard_map(
         steps,

time: 144 us -> 143 us (level)
  the two profiles are of different devices: /device:TPU:63 before, /device:TPU:93 now
where the time goes in v4:
time: 143 us; the launch traced here: 142 us
  starting transfers between devices  65 us (45%)
  waiting for transfers between devices  50.2 us (35%)
  Pallas kernels  22.1 us (15%)
  local copies, waits for them, and re-layouts  3.76 us (3%)
    ppermute x6, starting transfers between devices, send(): lax.ppermute(piece, 'y', [(y, (y + step) % ring) for y in range(ring)])  18.8 us
    all_to_all x1, starting transfers between devices, steps(): keys_g = lax.all_to_all(keys_g, SPREAD, 0, 0, tiled=True)  18.6 us
    all_to_all x1, starting transfers between devices, steps(): rows_p = lax.all_to_all(packed_p, SPREAD, 0, 0, tiled=True)  16.7 us
    ppermute x1, waiting for transfers between devices, steps(): came_p = lax.ppermute(sent_p, 'xh', pair)  15 us
    all_to_all x1, waiting for transfers between devices, steps(): rows_p = lax.all_to_all(packed_p, SPREAD, 0, 0, tiled=True)  10.6 us
    ppermute x1, waiting for transfers between devices, steps(): came_g = lax.ppermute(sent_g, 'xh', pair)  9.98 us
    pallas_call x2, Pallas kernels, project_sent(): pl.pallas_call(sent_kernel, out_shape=(jax.ShapeDtypeStruct((rows, 128),...  7.84 us
    ppermute x1, waiting for transfers between devices, steps(): mine = lax.ppermute(leaving, SUBCUBE, crossing())  7.31 us
  transfers between devices with their start and end apart: 12, of which 5 were waited for; matrix products, arithmetic and copies ran while one was open for 1% of the time, Pallas kernels for 11%

profile of v4, /device:TPU:93, one launch (start us, length us, event | category | flops | bytes accessed | tf_op | source)
XLA Modules:
  0.0 141.8 jit_solution(13021537244939018176)
XLA Ops:
  0.0 4.1 %pack.1 = (bf16[64,8,512]{2,1,0:T(8,128)(2,1)}, bf16[64,8,512]{2,1,0:T(8,128)(2,1)}, bf16[1024,512]{1,0:T(8,128)(2,1)}) custom-call(s32[8192]{0:T(1024)} %table.1, bf16[128,8,512]{2,1,0:T(8,128)(2,1)} %bitcast.58, bf16[4096,512]{1,0:T(8,128)(2,1)} %w_own.3), custom_call_target="tpu_custom_call" | custom-call | flops 17179869184 | tf_op jit(solution)/shard_map/pack/pallas_call | solution.py:121
  4.2 2.2 %collective-permute-start.3 = (bf16[1024,512]{1,0:T(8,128)(2,1)}, bf16[1024,512]{1,0:T(8,128)(2,1)S(1)}, u32[]{:S(2)}, u32[]{:S(2)}) collective-permute-start(bf16[1024,512]{1,0:T(8,128)(2,1)} %get-tuple-element.17), channel_id=1, source_target_pairs={{0,20},{4,16},{8,28},{12,24},{16,4},{20,0},{24,12},{28,8},{1,21},{... | collective-permute-start | bytes 3145736 | tf_op jit(solution)/shard_map/ppermute | solution.py:394
  6.3 16.7 %all-to-all-start = ((bf16[64,8,512]{2,1,0:T(8,128)(2,1)}), bf16[64,8,512]{2,1,0:T(8,128)(2,1)S(1)}, u32[]{:S(2)}, u32[]{:S(2)}) async-start(bf16[64,8,512]{2,1,0:T(8,128)(2,1)} %get-tuple-element.16), calls=%async_computation | async-start | bytes 1048576 | tf_op jit(solution)/shard_map/all_to_all | solution.py:397
  23.0 7.3 %collective-permute-done.3.w_mine = bf16[1024,512]{1,0:T(8,128)(2,1)S(1)} collective-permute-done((bf16[1024,512]{1,0:T(8,128)(2,1)}, bf16[1024,512]{1,0:T(8,128)(2,1)S(1)}, u32[]{:S(2)}, u32[]{:S(2)}) %collective-permute-start.3) | collective-permute-done | bytes 1048608 | tf_op jit(solution)/shard_map/ppermute | solution.py:394
  30.3 3.4 %collective-permute-start.4 = (bf16[1024,512]{1,0:T(8,128)(2,1)S(1)}, bf16[1024,512]{1,0:T(8,128)(2,1)S(1)}, u32[]{:S(2)}, u32[]{:S(2)}) collective-permute-start(bf16[1024,512]{1,0:T(8,128)(2,1)S(1)} %collective-permute-done.3.w_mine), channel_id=1, source_target_pairs={{0,8},{8,0},{1,9},{9,1},{2,10},{10,2},{3,11},{11,3},{4,12},{12,4},... | collective-permute-start | bytes 3145736 | tf_op jit(solution)/shard_map/ppermute | solution.py:395
  33.7 2.9 %collective-permute-start.6 = (bf16[512,512]{1,0:T(8,128)(2,1)}, bf16[512,512]{1,0:T(8,128)(2,1)S(1)}, u32[]{:S(2)}, u32[]{:S(2)}) collective-permute-start(bf16[512,512]{1,0:T(8,128)(2,1)} %bitcast.47), channel_id=1, source_target_pairs={{0,2},{1,3},{2,0},{3,1},{4,6},{5,7},{6,4},{7,5},{8,10},{9,11},{10,... | collective-permute-start | bytes 1572872 | tf_op jit(solution)/shard_map/ppermute | solution.py:39
  36.6 3.8 %collective-permute-start.7 = (bf16[512,512]{1,0:T(8,128)(2,1)}, bf16[512,512]{1,0:T(8,128)(2,1)}, u32[]{:S(2)}, u32[]{:S(2)}) collective-permute-start(bf16[512,512]{1,0:T(8,128)(2,1)} %bitcast.48), channel_id=1, source_target_pairs={{0,1},{1,2},{2,3},{3,0},{4,5},{5,6},{6,7},{7,4},{8,9},{9,10},{10,1... | collective-permute-start | bytes 1572872 | tf_op jit(solution)/shard_map/ppermute | solution.py:39
  40.4 1.9 %collective-permute-start.8 = (bf16[512,512]{1,0:T(8,128)(2,1)}, bf16[512,512]{1,0:T(8,128)(2,1)}, u32[]{:S(2)}, u32[]{:S(2)}) collective-permute-start(bf16[512,512]{1,0:T(8,128)(2,1)} %bitcast.49), channel_id=1, source_target_pairs={{0,3},{1,0},{2,1},{3,2},{4,7},{5,4},{6,5},{7,6},{8,11},{9,8},{10,9... | collective-permute-start | bytes 1572872 | tf_op jit(solution)/shard_map/ppermute | solution.py:39
  43.7 10.6 %all-to-all-done = bf16[64,8,512]{2,1,0:T(8,128)(2,1)S(1)} async-done(((bf16[64,8,512]{2,1,0:T(8,128)(2,1)}), bf16[64,8,512]{2,1,0:T(8,128)(2,1)S(1)}, u32[]{:S(2)}, u32[]{:S(2)}) %all-to-all-start) | async-done | bytes 524320 | tf_op jit(solution)/shard_map/all_to_all | solution.py:397
  54.3 2.9 %collective-permute-start = (bf16[512,512]{1,0:T(8,128)(2,1)S(1)}, bf16[512,512]{1,0:T(8,128)(2,1)}, u32[]{:S(2)}, u32[]{:S(2)}) collective-permute-start(bf16[512,512]{1,0:T(8,128)(2,1)S(1)} %bitcast.42), channel_id=1, source_target_pairs={{0,2},{1,3},{2,0},{3,1},{4,6},{5,7},{6,4},{7,5},{8,10},{9,11},{10,... | collective-permute-start | bytes 1572872 | tf_op jit(solution)/shard_map/ppermute | solution.py:39
  57.9 3.8 %collective-permute-start.1 = (bf16[512,512]{1,0:T(8,128)(2,1)S(1)}, bf16[512,512]{1,0:T(8,128)(2,1)}, u32[]{:S(2)}, u32[]{:S(2)}) collective-permute-start(bf16[512,512]{1,0:T(8,128)(2,1)S(1)} %bitcast.43), channel_id=1, source_target_pairs={{0,1},{1,2},{2,3},{3,0},{4,5},{5,6},{6,7},{7,4},{8,9},{9,10},{10,1... | collective-permute-start | bytes 1572872 | tf_op jit(solution)/shard_map/ppermute | solution.py:39
  61.8 3.6 %collective-permute-start.2 = (bf16[512,512]{1,0:T(8,128)(2,1)S(1)}, bf16[512,512]{1,0:T(8,128)(2,1)}, u32[]{:S(2)}, u32[]{:S(2)}) collective-permute-start(bf16[512,512]{1,0:T(8,128)(2,1)S(1)} %bitcast.44), channel_id=1, source_target_pairs={{0,3},{1,0},{2,1},{3,2},{4,7},{5,4},{6,5},{7,6},{8,11},{9,8},{10,9... | collective-permute-start | bytes 1572872 | tf_op jit(solution)/shard_map/ppermute | solution.py:39
  67.5 3.8 %shard_map.48 = (f32[512,128]{1,0:T(8,128)S(1)}, bf16[65,8,512]{2,1,0:T(8,128)(2,1)S(1)}) custom-call(bf16[512,512]{1,0:T(8,128)(2,1)S(1)} %bitcast.50, bf16[512,512]{1,0:T(8,128)(2,1)S(1)} %copy-done.5, bf16[512,512]{1,0:T(8,128)(2,1)} %collective-permute-done.7.p2, bf16[512,512]{1,0:T(8,128)(2,1)} %collective-permute-done.8.p3, f32[8,1,512]{2,1,0:T(1,128)S(1)} %bitcast.52, ...), custom_call_target="tpu_custom_call" | custom-call | flops 17179869184 | tf_op jit(solution)/shard_map/pallas_call | solution.py:234
  71.3 3.3 %collective-permute-start.9 = (bf16[65,8,512]{2,1,0:T(8,128)(2,1)S(1)}, bf16[65,8,512]{2,1,0:T(8,128)(2,1)S(1)}, u32[]{:S(2)}, u32[]{:S(2)}) collective-permute-start(bf16[65,8,512]{2,1,0:T(8,128)(2,1)S(1)} %get-tuple-element.25), channel_id=1, source_target_pairs={{0,4},{4,0},{1,5},{5,1},{2,6},{6,2},{3,7},{7,3},{8,12},{12,8},{9,1... | collective-permute-start | bytes 1597448 | tf_op jit(solution)/shard_map/ppermute | solution.py:405
  74.7 2.8 %shard_map.49 = (f32[512,512]{1,0:T(8,128)S(1)}, f32[8,512]{1,0:T(8,128)S(1)}) custom-call(s32[1]{0:T(128)} %bitcast.3.half_id, bf16[512,512]{1,0:T(8,128)(2,1)S(1)} %bitcast.51, bf16[512,512]{1,0:T(8,128)(2,1)S(1)} %copy-done.6, bf16[512,512]{1,0:T(8,128)(2,1)} %collective-permute-done.7.p2, bf16[512,512]{1,0:T(8,128)(2,1)} %collective-permute-done.8.p3, ...), custom_call_target="tpu_custom_call" | custom-call | flops 17179869184 | tf_op jit(solution)/shard_map/pallas_call | solution.py:277
  77.6 10.0 %collective-permute-done.9.came = bf16[65,8,512]{2,1,0:T(8,128)(2,1)S(1)} collective-permute-done((bf16[65,8,512]{2,1,0:T(8,128)(2,1)S(1)}, bf16[65,8,512]{2,1,0:T(8,128)(2,1)S(1)}, u32[]{:S(2)}, u32[]{:S(2)}) %collective-permute-start.9) | collective-permute-done | bytes 532512 | tf_op jit(solution)/shard_map/ppermute | solution.py:405
  87.5 1.7 %sum_g.1 = bf16[64,8,512]{2,1,0:T(8,128)(2,1)} custom-call(f32[512,512]{1,0:T(8,128)S(1)} %get-tuple-element.24.kept, f32[512,128]{1,0:T(8,128)S(1)} %get-tuple-element.23.table, bf16[65,8,512]{2,1,0:T(8,128)(2,1)S(1)} %collective-permute-done.9.came, f32[8,512]{1,0:T(8,128)S(1)} %get-tuple-element.26.gain_sums), custom_call_target="tpu_custom_call" | custom-call | flops 17179869184 | tf_op jit(solution)/shard_map/sum_g/pallas_call | solution.py:332
  89.2 18.6 %all-to-all-start.1 = ((bf16[64,8,512]{2,1,0:T(8,128)(2,1)}), bf16[64,8,512]{2,1,0:T(8,128)(2,1)S(1)}, u32[]{:S(2)}, u32[]{:S(2)}) async-start(bf16[64,8,512]{2,1,0:T(8,128)(2,1)} %sum_g.1), calls=%async_computation.1 | async-start | bytes 1048576 | tf_op jit(solution)/shard_map/all_to_all | solution.py:408
  107.9 4.0 %shard_map.46 = (f32[512,128]{1,0:T(8,128)S(1)}, bf16[65,8,512]{2,1,0:T(8,128)(2,1)S(1)}) custom-call(bf16[512,512]{1,0:T(8,128)(2,1)S(1)} %bitcast.45, bf16[512,512]{1,0:T(8,128)(2,1)} %collective-permute-done.p1, bf16[512,512]{1,0:T(8,128)(2,1)} %collective-permute-done.1.p2, bf16[512,512]{1,0:T(8,128)(2,1)} %collective-permute-done.2.p3, ...), custom_call_target="tpu_custom_call" | custom-call | flops 17179869184 | tf_op jit(solution)/shard_map/pallas_call | solution.py:234
  111.9 1.9 %collective-permute-start.5 = (bf16[65,8,512]{2,1,0:T(8,128)(2,1)S(1)}, bf16[65,8,512]{2,1,0:T(8,128)(2,1)S(1)}, u32[]{:S(2)}, u32[]{:S(2)}) collective-permute-start(bf16[65,8,512]{2,1,0:T(8,128)(2,1)S(1)} %get-tuple-element.20), channel_id=1, source_target_pairs={{0,4},{4,0},{1,5},{5,1},{2,6},{6,2},{3,7},{7,3},{8,12},{12,8},{9,1... | collective-permute-start | bytes 1597448 | tf_op jit(solution)/shard_map/ppermute | solution.py:412
  113.9 3.0 %shard_map.47 = (f32[512,512]{1,0:T(8,128)S(1)}, f32[8,512]{1,0:T(8,128)S(1)}) custom-call(s32[1]{0:T(128)} %bitcast.3.half_id, bf16[512,512]{1,0:T(8,128)(2,1)S(1)} %bitcast.46, bf16[512,512]{1,0:T(8,128)(2,1)} %collective-permute-done.p1, bf16[512,512]{1,0:T(8,128)(2,1)} %collective-permute-done.1.p2, bf16[512,512]{1,0:T(8,128)(2,1)} %collective-permute-done.2.p3, ...), custom_call_target="tpu_custom_call" | custom-call | flops 17179869184 | tf_op jit(solution)/shard_map/pallas_call | solution.py:277
  116.9 15.0 %collective-permute-done.5.came = bf16[65,8,512]{2,1,0:T(8,128)(2,1)S(1)} collective-permute-done((bf16[65,8,512]{2,1,0:T(8,128)(2,1)S(1)}, bf16[65,8,512]{2,1,0:T(8,128)(2,1)S(1)}, u32[]{:S(2)}, u32[]{:S(2)}) %collective-permute-start.5) | collective-permute-done | bytes 532512 | tf_op jit(solution)/shard_map/ppermute | solution.py:412
  131.9 7.3 %all-to-all-done.1.others = bf16[64,8,512]{2,1,0:T(8,128)(2,1)S(1)} async-done(((bf16[64,8,512]{2,1,0:T(8,128)(2,1)}), bf16[64,8,512]{2,1,0:T(8,128)(2,1)S(1)}, u32[]{:S(2)}, u32[]{:S(2)}) %all-to-all-start.1) | async-done | bytes 524320 | tf_op jit(solution)/shard_map/all_to_all | solution.py:408
  139.2 2.6 %place.1 = bf16[128,8,512]{2,1,0:T(8,128)(2,1)} custom-call(s32[128]{0:T(128)S(1)} %pad_add_fusion.slots, f32[512,512]{1,0:T(8,128)S(1)} %get-tuple-element.19.kept, f32[512,128]{1,0:T(8,128)S(1)} %get-tuple-element.18.table, bf16[65,8,512]{2,1,0:T(8,128)(2,1)S(1)} %collective-permute-done.5.came, f32[8,512]{1,0:T(8,128)S(1)} %get-tuple-element.21.gain_sums, ...), custom_call_target="tpu_custom_call" | custom-call | flops 17179869184 | tf_op jit(solution)/shard_map/place/pallas_call | solution.py:361
  (34 shorter events, 4.2 us)
Async XLA Ops:
  0.0 42.4 %copy-start.8 = (s32[8192]{0:T(1024)S(1)}, s32[8192]{0:T(1024)}, u32[]{:S(2)}) copy-start(s32[8192]{0:T(1024)} %table.1) | copy-start | bytes 98308
  0.0 65.4 %copy-start.7 = (f32[4096]{0:T(1024)S(1)}, f32[4096]{0:T(1024)}, u32[]{:S(2)}) copy-start(f32[4096]{0:T(1024)} %param.5) | copy-start | bytes 49156
  4.2 26.1 %collective-permute-start.3 = (bf16[1024,512]{1,0:T(8,128)(2,1)}, bf16[1024,512]{1,0:T(8,128)(2,1)S(1)}, u32[]{:S(2)}, u32[]{:S(2)}) collective-permute-start(bf16[1024,512]{1,0:T(8,128)(2,1)} %get-tuple-element.17), channel_id=1, source_target_pairs={{0,20},{4,16},{8,28},{12,24},{16,4},{20,0},{24,12},{28,8},{1,21},{... | collective-permute-start | bytes 3145736 | tf_op jit(solution)/shard_map/ppermute | solution.py:394
  6.3 47.9 %all-to-all-start = ((bf16[64,8,512]{2,1,0:T(8,128)(2,1)}), bf16[64,8,512]{2,1,0:T(8,128)(2,1)S(1)}, u32[]{:S(2)}, u32[]{:S(2)}) async-start(bf16[64,8,512]{2,1,0:T(8,128)(2,1)} %get-tuple-element.16), calls=%async_computation | async-start | bytes 1048576 | tf_op jit(solution)/shard_map/all_to_all | solution.py:397
  30.3 35.1 %collective-permute-start.4 = (bf16[1024,512]{1,0:T(8,128)(2,1)S(1)}, bf16[1024,512]{1,0:T(8,128)(2,1)S(1)}, u32[]{:S(2)}, u32[]{:S(2)}) collective-permute-start(bf16[1024,512]{1,0:T(8,128)(2,1)S(1)} %collective-permute-done.3.w_mine), channel_id=1, source_target_pairs={{0,8},{8,0},{1,9},{9,1},{2,10},{10,2},{3,11},{11,3},{4,12},{12,4},... | collective-permute-start | bytes 3145736 | tf_op jit(solution)/shard_map/ppermute | solution.py:395
  33.7 23.4 %collective-permute-start.6 = (bf16[512,512]{1,0:T(8,128)(2,1)}, bf16[512,512]{1,0:T(8,128)(2,1)S(1)}, u32[]{:S(2)}, u32[]{:S(2)}) collective-permute-start(bf16[512,512]{1,0:T(8,128)(2,1)} %bitcast.47), channel_id=1, source_target_pairs={{0,2},{1,3},{2,0},{3,1},{4,6},{5,7},{6,4},{7,5},{8,10},{9,11},{10,... | collective-permute-start | bytes 1572872 | tf_op jit(solution)/shard_map/ppermute | solution.py:39
  36.6 25.1 %collective-permute-start.7 = (bf16[512,512]{1,0:T(8,128)(2,1)}, bf16[512,512]{1,0:T(8,128)(2,1)}, u32[]{:S(2)}, u32[]{:S(2)}) collective-permute-start(bf16[512,512]{1,0:T(8,128)(2,1)} %bitcast.48), channel_id=1, source_target_pairs={{0,1},{1,2},{2,3},{3,0},{4,5},{5,6},{6,7},{7,4},{8,9},{9,10},{10,1... | collective-permute-start | bytes 1572872 | tf_op jit(solution)/shard_map/ppermute | solution.py:39
  40.4 24.9 %collective-permute-start.8 = (bf16[512,512]{1,0:T(8,128)(2,1)}, bf16[512,512]{1,0:T(8,128)(2,1)}, u32[]{:S(2)}, u32[]{:S(2)}) collective-permute-start(bf16[512,512]{1,0:T(8,128)(2,1)} %bitcast.49), channel_id=1, source_target_pairs={{0,3},{1,0},{2,1},{3,2},{4,7},{5,4},{6,5},{7,6},{8,11},{9,8},{10,9... | collective-permute-start | bytes 1572872 | tf_op jit(solution)/shard_map/ppermute | solution.py:39
  54.3 53.6 %collective-permute-start = (bf16[512,512]{1,0:T(8,128)(2,1)S(1)}, bf16[512,512]{1,0:T(8,128)(2,1)}, u32[]{:S(2)}, u32[]{:S(2)}) collective-permute-start(bf16[512,512]{1,0:T(8,128)(2,1)S(1)} %bitcast.42), channel_id=1, source_target_pairs={{0,2},{1,3},{2,0},{3,1},{4,6},{5,7},{6,4},{7,5},{8,10},{9,11},{10,... | collective-permute-start | bytes 1572872 | tf_op jit(solution)/shard_map/ppermute | solution.py:39
  57.1 0.8 copy-start.4
  57.9 50.0 %collective-permute-start.1 = (bf16[512,512]{1,0:T(8,128)(2,1)S(1)}, bf16[512,512]{1,0:T(8,128)(2,1)}, u32[]{:S(2)}, u32[]{:S(2)}) collective-permute-start(bf16[512,512]{1,0:T(8,128)(2,1)S(1)} %bitcast.43), channel_id=1, source_target_pairs={{0,1},{1,2},{2,3},{3,0},{4,5},{5,6},{6,7},{7,4},{8,9},{9,10},{10,1... | collective-permute-start | bytes 1572872 | tf_op jit(solution)/shard_map/ppermute | solution.py:39
  61.8 46.2 %collective-permute-start.2 = (bf16[512,512]{1,0:T(8,128)(2,1)S(1)}, bf16[512,512]{1,0:T(8,128)(2,1)}, u32[]{:S(2)}, u32[]{:S(2)}) collective-permute-start(bf16[512,512]{1,0:T(8,128)(2,1)S(1)} %bitcast.44), channel_id=1, source_target_pairs={{0,3},{1,0},{2,1},{3,2},{4,7},{5,4},{6,5},{7,6},{8,11},{9,8},{10,9... | collective-permute-start | bytes 1572872 | tf_op jit(solution)/shard_map/ppermute | solution.py:39
  65.4 1.0 copy-start.2
  66.4 1.0 copy-start.5
  67.5 7.2 %copy-start = (bf16[4096,512]{1,0:T(8,128)(2,1)S(1)}, bf16[4096,512]{1,0:T(8,128)(2,1)}, u32[]{:S(2)}) copy-start(bf16[4096,512]{1,0:T(8,128)(2,1)} %w_own.3) | copy-start | bytes 12582916
  67.5 7.2 %copy-start.3 = (bf16[64,8,512]{2,1,0:T(8,128)(2,1)S(1)}, bf16[64,8,512]{2,1,0:T(8,128)(2,1)}, u32[]{:S(2)}) copy-start(bf16[64,8,512]{2,1,0:T(8,128)(2,1)} %get-tuple-element.22) | copy-start | bytes 1572868
  67.5 7.2 %copy-start.6 = (bf16[512,512]{1,0:T(8,128)(2,1)S(1)}, bf16[512,512]{1,0:T(8,128)(2,1)}, u32[]{:S(2)}) copy-start(bf16[512,512]{1,0:T(8,128)(2,1)} %copy-done.4) | copy-start | bytes 1572868
  71.3 16.2 %collective-permute-start.9 = (bf16[65,8,512]{2,1,0:T(8,128)(2,1)S(1)}, bf16[65,8,512]{2,1,0:T(8,128)(2,1)S(1)}, u32[]{:S(2)}, u32[]{:S(2)}) collective-permute-start(bf16[65,8,512]{2,1,0:T(8,128)(2,1)S(1)} %get-tuple-element.25), channel_id=1, source_target_pairs={{0,4},{4,0},{1,5},{5,1},{2,6},{6,2},{3,7},{7,3},{8,12},{12,8},{9,1... | collective-permute-start | bytes 1597448 | tf_op jit(solution)/shard_map/ppermute | solution.py:405
  89.2 49.9 %all-to-all-start.1 = ((bf16[64,8,512]{2,1,0:T(8,128)(2,1)}), bf16[64,8,512]{2,1,0:T(8,128)(2,1)S(1)}, u32[]{:S(2)}, u32[]{:S(2)}) async-start(bf16[64,8,512]{2,1,0:T(8,128)(2,1)} %sum_g.1), calls=%async_computation.1 | async-start | bytes 1048576 | tf_op jit(solution)/shard_map/all_to_all | solution.py:408
  107.9 6.0 %copy-start.1 = (bf16[4096,512]{1,0:T(8,128)(2,1)S(1)}, bf16[4096,512]{1,0:T(8,128)(2,1)}, u32[]{:S(2)}) copy-start(bf16[4096,512]{1,0:T(8,128)(2,1)} %w_own.3) | copy-start | bytes 12582916
  111.9 20.0 %collective-permute-start.5 = (bf16[65,8,512]{2,1,0:T(8,128)(2,1)S(1)}, bf16[65,8,512]{2,1,0:T(8,128)(2,1)S(1)}, u32[]{:S(2)}, u32[]{:S(2)}) collective-permute-start(bf16[65,8,512]{2,1,0:T(8,128)(2,1)S(1)} %get-tuple-element.20), channel_id=1, source_target_pairs={{0,4},{4,0},{1,5},{5,1},{2,6},{6,2},{3,7},{7,3},{8,12},{12,8},{9,1... | collective-permute-start | bytes 1597448 | tf_op jit(solution)/shard_map/ppermute | solution.py:412
